TPU v7x, 32 devices: a whole 2x2x4 slice. The times are simulated.
32 devices in a mesh: dp: 8 (over y, x, core), tensor: 4 (over z).
Axes of the slice: x: 2, y: 2, z: 4, core: 2. Of those that a mesh axis runs over, the one named last changes fastest.
Arguments:
- block_in: bfloat16 [12288, 1536], P(('dp', 'tensor')), may hold values from -6 to 6
- cotangent: bfloat16 [12288, 1536], P(('dp', 'tensor')), may hold values from -6 to 6
- segment_ids: int32 [24, 512], P('dp'), may hold values from 0 to 3, never falling along the last dimension, each value on 1 to 256 neighbouring positions
- attn_gain: bfloat16 [1536], P('dp'), may hold values from 0.5 to 1.5
- qkv_weight: bfloat16 [1536, 3072], P('dp', 'tensor'), may hold values from -4 to 4
- out_weight: bfloat16 [1536, 1536], P('tensor', 'dp'), may hold values from -1.25 to 1.25
- mlp_gain: bfloat16 [1536], P('dp'), may hold values from 0.5 to 1.5
- gate_weight: bfloat16 [1536, 4096], P('dp', 'tensor'), may hold values from -0.15625 to 0.15625
- up_weight: bfloat16 [1536, 4096], P('dp', 'tensor'), may hold values from -0.15625 to 0.15625
- down_weight: bfloat16 [4096, 1536], P('tensor', 'dp'), may hold values from -0.09375 to 0.09375
Outputs:
- block_out: bfloat16 [12288, 1536], P(('dp', 'tensor'))
- input_grad: bfloat16 [12288, 1536], P(('dp', 'tensor'))
- attn_gain_grad: float32 [1536], P('dp')
- qkv_grad: float32 [1536, 3072], P('dp', 'tensor')
- out_grad: float32 [1536, 1536], P('tensor', 'dp')
- mlp_gain_grad: float32 [1536], P('dp')
- gate_grad: float32 [1536, 4096], P('dp', 'tensor')
- up_grad: float32 [1536, 4096], P('dp', 'tensor')
- down_grad: float32 [4096, 1536], P('tensor', 'dp')
Inputs may be any that keep to these rules, and one draw needn't show every extreme that they name: `segment_ids`: segment numbers never fall along a sequence; a segment holds at most 256 tokens of its sequence, and some segment of every sequence holds exactly that many.
All inputs are finite; a program needn't handle non-finite values.
Results may differ from a plain program's by a relative error of at most 0.025.
The roundings to bfloat16 on the way count: a program that leaves them out, or rounds other values in their place, can miss the bound.
Values may be sent and summed in bfloat16 or wider, within the bound.
A program may use at most 192 MiB of HBM per device.

v0:
```python
import jax
import jax.numpy as jnp
from jax import lax
from jax.sharding import PartitionSpec as P

QUERY_HEADS = 16
KEY_VALUE_HEADS = 8
HEAD_SIZE = 96


EPS = 1e-05
ROPE_BASE = 100000.0
NEG_FILL = -1e30


def doc_positions(segments):
    length = segments.shape[1]
    position_index = jnp.broadcast_to(jnp.arange(length, dtype=jnp.int32)[None, :], segments.shape)
    change = jnp.concatenate(
        [jnp.ones((segments.shape[0], 1), dtype=bool), segments[:, 1:] != segments[:, :-1]], axis=1
    )
    starts = lax.cummax(jnp.where(change, position_index, jnp.zeros_like(position_index)), axis=1)
    return position_index - starts


def rotary_tables(segments):
    half_dim = HEAD_SIZE // 2
    frequency = jnp.power(ROPE_BASE, -(2.0 * jnp.arange(half_dim, dtype=jnp.float32)) / HEAD_SIZE)
    angles = doc_positions(segments).astype(jnp.float32)[..., None] * frequency
    cosine_table = jnp.concatenate([jnp.cos(angles), jnp.cos(angles)], axis=-1)
    sine_table = jnp.concatenate([jnp.sin(angles), jnp.sin(angles)], axis=-1)
    return (cosine_table, sine_table)


def rotate(vector, cosine_table, sine_table):
    half_dim = vector.shape[-1] // 2
    turned = jnp.concatenate([-vector[..., half_dim:], vector[..., :half_dim]], axis=-1)
    return vector * cosine_table + turned * sine_table


def unrotate(vector, cosine_table, sine_table):
    half_dim = vector.shape[-1] // 2
    shifted = vector * sine_table
    returned = jnp.concatenate([shifted[..., half_dim:], -shifted[..., :half_dim]], axis=-1)
    return vector * cosine_table + returned


def allowed_pairs(segments):
    length = segments.shape[1]
    offsets = jnp.arange(length)
    causal = offsets[None, :] <= offsets[:, None]
    same_doc = segments[:, :, None] == segments[:, None, :]
    return (causal[None] & same_doc)[:, None, None]


def score_block(queries, key_heads, segments):
    scores = jnp.einsum(
        "sqgrd,skgd->sgrqk", queries, key_heads, preferred_element_type=jnp.float32
    ) * HEAD_SIZE ** (-0.5)
    return jnp.where(allowed_pairs(segments), scores, NEG_FILL)


def rms_scale(features):
    return lax.rsqrt(jnp.mean(features * features, axis=-1, keepdims=True) + EPS)


def norm_back(features, inverse, gain_vector, upstream):
    scaled = gain_vector * upstream
    return inverse * scaled - features * (inverse * inverse * inverse) * jnp.mean(
        scaled * features, axis=-1, keepdims=True
    )


def widen(shard_rows):
    return lax.all_gather(shard_rows, "tensor", axis=0, tiled=True)


def narrow(partial_value):
    return lax.psum_scatter(
        partial_value.astype(jnp.bfloat16), "tensor", scatter_dimension=0, tiled=True
    ).astype(jnp.float32)


def local(
    block_in,
    cotangent,
    segment_ids,
    attn_gain,
    qkv_weight,
    out_weight,
    mlp_gain,
    gate_weight,
    up_weight,
    down_weight,
):
    qkv_full, gate_full, up_full, gain_attn_raw, gain_mlp_raw = (
        lax.all_gather(qkv_weight, "dp", axis=0, tiled=True),
        lax.all_gather(gate_weight, "dp", axis=0, tiled=True),
        lax.all_gather(up_weight, "dp", axis=0, tiled=True),
        lax.all_gather(attn_gain, "dp", axis=0, tiled=True),
        lax.all_gather(mlp_gain, "dp", axis=0, tiled=True),
    )
    out_cols, down_cols = (
        lax.all_gather(out_weight, "dp", axis=1, tiled=True),
        lax.all_gather(down_weight, "dp", axis=1, tiled=True),
    )
    seq_count, length = segment_ids.shape
    repeat_factor = QUERY_HEADS // KEY_VALUE_HEADS
    groups = qkv_full.shape[1] // ((repeat_factor + 2) * HEAD_SIZE)
    gain_attn = gain_attn_raw.astype(jnp.float32)
    gain_mlp = gain_mlp_raw.astype(jnp.float32)
    residual = block_in.astype(jnp.float32)
    scale_attn = rms_scale(residual)
    normed1 = widen((residual * scale_attn * gain_attn).astype(jnp.bfloat16))
    projected = jnp.dot(normed1, qkv_full, preferred_element_type=jnp.float32).reshape(
        seq_count, length, groups, repeat_factor + 2, HEAD_SIZE
    )
    cosine_table, sine_table = rotary_tables(segment_ids)
    cos_query = cosine_table[:, :, None, None, :]
    sin_query = sine_table[:, :, None, None, :]
    cos_key = cosine_table[:, :, None, :]
    sin_key = sine_table[:, :, None, :]
    queries = rotate(projected[:, :, :, :repeat_factor], cos_query, sin_query).astype(jnp.bfloat16)
    key_heads = rotate(projected[:, :, :, repeat_factor], cos_key, sin_key).astype(jnp.bfloat16)
    values = projected[:, :, :, repeat_factor + 1].astype(jnp.bfloat16)
    scores = score_block(queries, key_heads, segment_ids)
    highest = jnp.max(scores, axis=-1, keepdims=True)
    log_total = highest + jnp.log(jnp.sum(jnp.exp(scores - highest), axis=-1, keepdims=True))
    probability = jnp.exp(scores - log_total).astype(jnp.bfloat16)
    attended = jnp.einsum(
        "sgrqk,skgd->sqgrd", probability, values, preferred_element_type=jnp.float32
    ).astype(jnp.bfloat16)
    attn_flat = attended.reshape(seq_count * length, groups * repeat_factor * HEAD_SIZE)
    attn_delta = lax.psum_scatter(
        jnp.dot(attn_flat, out_cols, preferred_element_type=jnp.float32).astype(jnp.bfloat16),
        "tensor",
        scatter_dimension=0,
        tiled=True,
    ).astype(jnp.float32)
    hidden1 = residual + attn_delta
    scale_mlp = rms_scale(hidden1)
    normed2 = widen((hidden1 * scale_mlp * gain_mlp).astype(jnp.bfloat16))
    gate = jnp.dot(normed2, gate_full, preferred_element_type=jnp.float32)
    up_value = jnp.dot(normed2, up_full, preferred_element_type=jnp.float32)
    sigmoid_gate = jax.nn.sigmoid(gate)
    activated = (gate * sigmoid_gate * up_value).astype(jnp.bfloat16)
    mlp_delta = narrow(jnp.dot(activated, down_cols, preferred_element_type=jnp.float32))
    block_out = (hidden1 + mlp_delta).astype(jnp.bfloat16)
    grad_rows = widen(cotangent)
    down_part = jnp.einsum("tf,td->fd", activated, grad_rows, preferred_element_type=jnp.float32)
    act_grad = jnp.einsum("td,fd->tf", grad_rows, down_cols, preferred_element_type=jnp.float32)
    gate_delta = (act_grad * up_value * sigmoid_gate * (1.0 + gate * (1.0 - sigmoid_gate))).astype(
        jnp.bfloat16
    )
    up_delta = (act_grad * gate * sigmoid_gate).astype(jnp.bfloat16)
    gate_part = jnp.einsum("td,tf->df", normed2, gate_delta, preferred_element_type=jnp.float32)
    up_part = jnp.einsum("td,tf->df", normed2, up_delta, preferred_element_type=jnp.float32)
    normed2_term = jnp.einsum(
        "tf,df->td", gate_delta, gate_full, preferred_element_type=jnp.float32
    ) + jnp.einsum("tf,df->td", up_delta, up_full, preferred_element_type=jnp.float32)
    normed2_grad = narrow(normed2_term)
    mlp_gain_part = jnp.sum(normed2_grad * hidden1 * scale_mlp, axis=0)
    hidden1_grad = cotangent.astype(jnp.float32) + norm_back(
        hidden1, scale_mlp, gain_mlp, normed2_grad
    )
    hidden1_rounded = hidden1_grad.astype(jnp.bfloat16)
    grad_full = lax.all_gather(hidden1_rounded, "tensor", axis=0, tiled=True)
    attended_grad = jnp.einsum(
        "td,hd->th", grad_full, out_cols, preferred_element_type=jnp.float32
    ).astype(jnp.bfloat16)
    out_part = jnp.einsum("th,td->hd", attn_flat, grad_full, preferred_element_type=jnp.float32)
    attended_grad = attended_grad.reshape(seq_count, length, groups, repeat_factor, HEAD_SIZE)
    prob_full = jnp.exp(score_block(queries, key_heads, segment_ids) - log_total)
    prob_grad = jnp.einsum(
        "sqgrd,skgd->sgrqk", attended_grad, values, preferred_element_type=jnp.float32
    )
    inner_sum = jnp.sum(prob_full * prob_grad, axis=-1, keepdims=True)
    score_grad = (prob_full * (prob_grad - inner_sum) * HEAD_SIZE ** (-0.5)).astype(jnp.bfloat16)
    query_grad = jnp.einsum(
        "sgrqk,skgd->sqgrd", score_grad, key_heads, preferred_element_type=jnp.float32
    )
    key_grad = jnp.einsum(
        "sgrqk,sqgrd->skgd", score_grad, queries, preferred_element_type=jnp.float32
    )
    value_grad = jnp.einsum(
        "sgrqk,sqgrd->skgd",
        prob_full.astype(jnp.bfloat16),
        attended_grad,
        preferred_element_type=jnp.float32,
    )
    projected_grad = jnp.concatenate(
        [
            unrotate(query_grad, cos_query, sin_query),
            unrotate(key_grad, cos_key, sin_key)[:, :, :, None],
            value_grad[:, :, :, None],
        ],
        axis=3,
    )
    projected_grad = projected_grad.astype(jnp.bfloat16).reshape(
        seq_count * length, groups * (repeat_factor + 2) * HEAD_SIZE
    )
    qkv_part = jnp.einsum("td,tc->dc", normed1, projected_grad, preferred_element_type=jnp.float32)
    normed1_grad = narrow(
        jnp.einsum("tc,dc->td", projected_grad, qkv_full, preferred_element_type=jnp.float32)
    )
    attn_gain_part = jnp.sum(normed1_grad * residual * scale_attn, axis=0)
    input_grad = (hidden1_grad + norm_back(residual, scale_attn, gain_attn, normed1_grad)).astype(
        jnp.bfloat16
    )
    attn_gain_total, mlp_gain_total = lax.psum((attn_gain_part, mlp_gain_part), "tensor")
    attn_gain_grad, qkv_grad, gate_grad, up_grad, mlp_gain_grad = (
        lax.psum_scatter(
            attn_gain_total.astype(jnp.bfloat16), "dp", scatter_dimension=0, tiled=True
        ).astype(jnp.float32),
        lax.psum_scatter(
            qkv_part.astype(jnp.bfloat16), "dp", scatter_dimension=0, tiled=True
        ).astype(jnp.float32),
        lax.psum_scatter(
            gate_part.astype(jnp.bfloat16), "dp", scatter_dimension=0, tiled=True
        ).astype(jnp.float32),
        lax.psum_scatter(
            up_part.astype(jnp.bfloat16), "dp", scatter_dimension=0, tiled=True
        ).astype(jnp.float32),
        lax.psum_scatter(
            mlp_gain_total.astype(jnp.bfloat16), "dp", scatter_dimension=0, tiled=True
        ).astype(jnp.float32),
    )
    out_grad, down_grad = (
        lax.psum_scatter(
            out_part.astype(jnp.bfloat16), "dp", scatter_dimension=1, tiled=True
        ).astype(jnp.float32),
        lax.psum_scatter(
            down_part.astype(jnp.bfloat16), "dp", scatter_dimension=1, tiled=True
        ).astype(jnp.float32),
    )
    return (
        block_out,
        input_grad,
        attn_gain_grad,
        qkv_grad,
        out_grad,
        mlp_gain_grad,
        gate_grad,
        up_grad,
        down_grad,
    )


def solution(mesh):
    in_specs = (
        P(("dp", "tensor"), None),
        P(("dp", "tensor"), None),
        P("dp", None),
        P("dp"),
        P("dp", "tensor"),
        P("tensor", "dp"),
        P("dp"),
        P("dp", "tensor"),
        P("dp", "tensor"),
        P("tensor", "dp"),
    )
    out_specs = (
        P(("dp", "tensor"), None),
        P(("dp", "tensor"), None),
        P("dp"),
        P("dp", "tensor"),
        P("tensor", "dp"),
        P("dp"),
        P("dp", "tensor"),
        P("dp", "tensor"),
        P("tensor", "dp"),
    )
    return jax.shard_map(local, mesh=mesh, in_specs=in_specs, out_specs=out_specs, check_vma=False)
```

profile of v0, /device:TPU:0, one launch (start us, length us, event | category | flops | bytes accessed | tf_op | source)
XLA Modules:
  0.0 1224.1 jit_solution(13426383904669908466)
XLA Ops:
  11.7 15.8 %all-reduce.7 = (bf16[1536]{0:T(1024)(128)(2,1)S(1)}, bf16[1536]{0:T(1024)(128)(2,1)S(1)}) all-reduce(bf16[1536]{0:T(1024)(128)(2,1)S(1)} %dynamic-update-slice, bf16[1536]{0:T(1024)(128)(2,1)S(1)} %dynamic-update-slice.1), channel_id=1, replica_groups=mesh['dp'=8,'tensor'=4] {'dp'}, use_global_device_ids=true, to_apply=%add.1 | all-reduce | flops 3072 | bytes 12288
  29.7 2.6 fusion.19
  37.5 4.1 all-gather.12.cloned.1.call-done
  41.7 91.6 %all-gather.10.cloned.1.call-done = bf16[1536,1536]{1,0:T(8,128)(2,1)} async-done(((bf16[384,1536]{1,0:T(8,128)(2,1)}), bf16[1536,1536]{1,0:T(8,128)(2,1)}) %all-gather.10.cloned.1.call-update) | async-done | bytes 4718608 | tf_op jit(solution)/shard_map/all_gather | solution.py:75
  133.3 9.2 fusion.62
  142.4 8.6 reshape.132
  151.1 4.4 slice.63
  155.5 5.6 slice.64
  161.1 5.5 slice.68
  166.6 11.5 fusion.58
  178.1 3.2 copy.67
  181.3 3.4 copy.68
  185.8 5.5 copy.64
  191.3 5.2 copy.65
  196.5 2.5 neg.24
  199.0 5.6 copy.66
  206.9 2.3 fusion.25
  209.2 2.6 fusion.5
  211.8 2.8 exponential_reduce_fusion
  216.3 4.3 fusion.30
  220.6 3.5 copy.49
  225.2 5.9 convolution_convert_fusion.2
  231.8 83.4 %reduce-scatter.10.cloned.1.call-done = bf16[384,1536]{1,0:T(8,128)(2,1)} async-done(((bf16[1536,1536]{1,0:T(8,128)(2,1)}), bf16[384,1536]{1,0:T(8,128)(2,1)}) %reduce-scatter.10.cloned.1.call-update) | async-done | bytes 1179664 | tf_op jit(solution)/shard_map/reduce_scatter | solution.py:134
  320.8 28.9 %all-gather.20.cloned.1.call-done = bf16[1536,1024]{1,0:T(8,128)(2,1)} async-done(((bf16[192,1024]{1,0:T(8,128)(2,1)}), bf16[1536,1024]{1,0:T(8,128)(2,1)}) %all-gather.20.cloned.1.call-update) | async-done | bytes 3145744 | tf_op jit(solution)/shard_map/all_gather | solution.py:99
  349.7 91.4 %all-gather.16.cloned.1.call-done = bf16[1536,1536]{1,0:T(8,128)(2,1)} async-done(((bf16[384,1536]{1,0:T(8,128)(2,1)}), bf16[1536,1536]{1,0:T(8,128)(2,1)}) %all-gather.16.cloned.1.call-update) | async-done | bytes 4718608 | tf_op jit(solution)/shard_map/all_gather | solution.py:75
  441.1 10.0 fusion.64
  451.1 22.5 %all-gather.18.cloned.1.call-done = bf16[1536,1024]{1,0:T(8,128)(2,1)} async-done(((bf16[192,1024]{1,0:T(8,128)(2,1)}), bf16[1536,1024]{1,0:T(8,128)(2,1)}) %all-gather.18.cloned.1.call-update) | async-done | bytes 3145744 | tf_op jit(solution)/shard_map/all_gather | solution.py:98
  473.6 9.7 fusion.63
  483.4 24.4 %all-gather.22.cloned.1.call-done = bf16[1024,1536]{0,1:T(8,128)(2,1)} async-done(((bf16[1024,192]{0,1:T(8,128)(2,1)}), bf16[1024,1536]{0,1:T(8,128)(2,1)}) %all-gather.22.cloned.1.call-update) | async-done | bytes 3145744 | tf_op jit(solution)/shard_map/all_gather | solution.py:105
  507.7 91.0 %all-gather.24.cloned.1.call-done = bf16[1536,1536]{1,0:T(8,128)(2,1)} async-done(((bf16[384,1536]{1,0:T(8,128)(2,1)}), bf16[1536,1536]{1,0:T(8,128)(2,1)}) %all-gather.24.cloned.1.call-update) | async-done | bytes 4718608 | tf_op jit(solution)/shard_map/all_gather | solution.py:75
  598.7 14.1 %multiply_convert_fusion = (bf16[1536,1024]{1,0:T(8,128)(2,1)S(1)}, bf16[1536,1024]{1,0:T(8,128)(2,1)S(1)}, bf16[1536,1024]{1,0:T(8,128)(2,1)}) fusion(f32[1536,1024]{1,0:T(8,128)} %fusion.63, f32[1536,1024]{1,0:T(8,128)} %fusion.64, bf16[1536,1536]{1,0:T(8,128)(2,1)} %all-gather.24.cloned.1.call-done, bf16[1024,1536]{0,1:T(8,128)(2,1)} %all-gather.22.cloned.1.call-done), kind=kOutput, calls=%fused_computation.15 | convolution fusion | flops 4857004032 | bytes 29884416 | tf_op jit(solution)/shard_map/td,fd->tf/dot_general | solution.py:151
  612.8 5.1 fusion.65
  618.0 7.4 add_convert_fusion
  625.5 83.8 %reduce-scatter.14.cloned.1.call-done = bf16[384,1536]{1,0:T(8,128)(2,1)} async-done(((bf16[1536,1536]{1,0:T(8,128)(2,1)}), bf16[384,1536]{1,0:T(8,128)(2,1)}) %reduce-scatter.14.cloned.1.call-update) | async-done | bytes 1179664 | tf_op jit(solution)/shard_map/reduce_scatter | solution.py:79
  709.3 2.8 fusion.16
  714.7 9.3 convolution_convert_fusion.3
  724.1 9.8 convolution_convert_fusion.4
  734.0 9.4 convolution_convert_fusion.5
  743.4 61.3 %all-gather.26.cloned.1.call-done = bf16[1536,1536]{1,0:T(8,128)(2,1)} async-done(((bf16[384,1536]{1,0:T(8,128)(2,1)}), bf16[1536,1536]{1,0:T(8,128)(2,1)}) %all-gather.26.cloned.1.call-update) | async-done | bytes 4718608 | tf_op jit(solution)/shard_map/all_gather | solution.py:167
  804.8 6.0 convolution_convert_fusion.8
  810.7 6.2 reshape.136
  816.9 4.8 copy.50
  821.7 7.8 fusion.39
  829.5 21.1 %broadcast_multiply_fusion = (f32[3,512,2,96]{1,3,2,0:T(8,128)}, f32[3,512,2,96]{1,3,2,0:T(8,128)}) fusion(f32[3,512,96]{1,2,0:T(8,128)S(1)} %copy-done.12, bf16[3,512,2,2,96]{1,4,3,2,0:T(8,128)(2,1)} %copy-done.17, f32[3,2,512,512,2]{3,2,4,1,0:T(8,128)} %fusion.39, f32[3,2,512,512,2]{3,2,4,1,0:T(8,128)} %copy-done.1, f32[3,2,2,512]{3,2,1,0:T(2,128)} %copy-done.30, ...), kind=kOutput, calls=%fused_computation.89 | convolution fusion | flops 638884352 | bytes 30105600 | tf_op jit(solution)/shard_map/sgrqk,sqgrd->skgd/dot_general | solution.py:182
  850.6 2.4 fusion.60
  853.0 25.2 %bitcast_multiply_fusion.1 = (f32[3,512,2,2,96]{1,4,3,2,0:T(8,128)}, f32[3,2,96,2,512]{4,2,3,1,0:T(8,128)}) fusion(f32[3,512,96]{1,2,0:T(8,128)S(1)} %copy-done.12, bf16[3,512,2,96,1]{1,3,4,2,0:T(8,128)(2,1)S(1)} %copy-done.21, f32[3,2,512,512,2]{3,2,4,1,0:T(8,128)} %fusion.39, f32[3,2,512,512,2]{3,2,4,1,0:T(8,128)} %copy-done.1, ...), kind=kOutput, calls=%fused_computation.59 | convolution fusion | flops 639179264 | bytes 31875072 | tf_op jit(solution)/shard_map/sgrqk,skgd->sqgrd/dot_general | solution.py:179
  878.2 3.6 fusion.59
  881.8 6.2 convolution_convert_fusion.7
  890.5 2.5 fusion.26
  893.0 6.8 fusion.33
  901.4 5.7 copy.55
  907.1 6.6 convert_element_type.166
  913.7 8.9 convolution_convert_fusion.6
  922.7 8.4 convolution_convert_fusion.1
  931.4 9.3 convolution_convert_fusion
  945.5 5.8 reduce-scatter.22.cloned.1.call-done
  953.3 37.9 %reduce-scatter.20.cloned.1.call-done = bf16[384,192]{0,1:T(8,128)(2,1)} async-done(((bf16[384,1536]{0,1:T(8,128)(2,1)}), bf16[384,192]{0,1:T(8,128)(2,1)}) %reduce-scatter.20.cloned.1.call-update) | async-done | bytes 147472 | tf_op jit(solution)/shard_map/reduce_scatter | solution.py:229
  992.8 43.9 %reduce-scatter.18.cloned.1.call-done = bf16[192,768]{1,0:T(8,128)(2,1)} async-done(((bf16[1536,768]{1,0:T(8,128)(2,1)}), bf16[192,768]{1,0:T(8,128)(2,1)}) %reduce-scatter.18.cloned.1.call-update) | async-done | bytes 294928 | tf_op jit(solution)/shard_map/reduce_scatter | solution.py:215
  1038.5 85.7 %reduce-scatter.16.cloned.1.call-done = bf16[384,1536]{1,0:T(8,128)(2,1)} async-done(((bf16[1536,1536]{1,0:T(8,128)(2,1)}), bf16[384,1536]{1,0:T(8,128)(2,1)}) %reduce-scatter.16.cloned.1.call-update) | async-done | bytes 1179664 | tf_op jit(solution)/shard_map/reduce_scatter | solution.py:79
  1124.2 2.6 fusion.23
  1126.8 19.9 %all-reduce.5 = (bf16[1536]{0:T(1024)(128)(2,1)}, bf16[1536]{0:T(1024)(128)(2,1)}) all-reduce(f32[1536]{0:T(1024)} %get-tuple-element.11, f32[1536]{0:T(1024)} %get-tuple-element.9), channel_id=1, replica_groups=mesh['dp'=8,'tensor'=4] {'tensor'}, use_global_device_ids=true, to_apply=%region_14.15 | all-reduce | flops 3072 | bytes 18432 | tf_op jit(solution)/shard_map/psum | solution.py:210
  1146.7 13.2 %all-reduce.6 = (bf16[1536]{0:T(1024)(128)(2,1)}, bf16[1536]{0:T(1024)(128)(2,1)}) all-reduce(bf16[1536]{0:T(1024)(128)(2,1)} %get-tuple-element.13, bf16[1536]{0:T(1024)(128)(2,1)} %get-tuple-element.14), channel_id=6, replica_groups=mesh['dp'=8,'tensor'=4] {'dp'}, use_global_device_ids=true, to_apply=%region_15.16.clone | all-reduce | flops 3072 | bytes 12288
  1163.8 48.7 %reduce-scatter.12.cloned.1.call-done = bf16[384,1536]{1,0:T(8,128)(2,1)} async-done(((bf16[1536,1536]{1,0:T(8,128)(2,1)}), bf16[384,1536]{1,0:T(8,128)(2,1)}) %reduce-scatter.12.cloned.1.call-update) | async-done | bytes 1179664 | tf_op jit(solution)/shard_map/reduce_scatter | solution.py:79
  1212.5 4.5 fusion.11
  (158 shorter events, 44.1 us)
Async XLA Ops:
  7.2 26.1 %copy-start.27 = (s32[3,512]{1,0:T(4,128)S(1)}, s32[3,512]{1,0:T(4,128)}, u32[]{:S(2)}) copy-start(s32[3,512]{1,0:T(4,128)} %param.12) | copy-start | bytes 18436
  7.2 34.5 %all-gather.12.cloned.1.call-start = ((), (), s32[]{:S(2)}) async-start(), calls=%async_computation.10 | async-start | bytes 2654208 | tf_op jit(solution)/shard_map/all_gather | solution.py:97
  7.9 125.3 %all-gather.10.cloned.1.call-start = ((), (), s32[]{:S(2)}) async-start(), calls=%async_computation.9 | async-start | bytes 5898240 | tf_op jit(solution)/shard_map/all_gather | solution.py:75
  27.5 5.6 copy-start.25
  29.7 3.4 copy-start.29
  32.3 192.9 %all-gather.14.cloned.1.call-start = ((), (), s32[]{:S(2)}) async-start(), calls=%async_computation.11 | async-start | bytes 1327104 | tf_op jit(solution)/shard_map/all_gather | solution.py:104
  33.1 282.2 %reduce-scatter.10.cloned.1.call-start = ((), (), s32[]{:S(2)}) async-start(), calls=%async_computation.12 | async-start | bytes 5898240 | tf_op jit(solution)/shard_map/reduce_scatter | solution.py:134
  35.5 179.2 %copy-start.9 = (pred[3,512,512]{1,2,0:T(8,128)(4,1)}, pred[3,512,512]{1,2,0:T(8,128)(4,1)S(1)}, u32[]{:S(2)}) copy-start(pred[3,512,512]{1,2,0:T(8,128)(4,1)S(1)} %compare_and_fusion) | copy-start | bytes 2359300
  37.5 168.9 %copy-start.3 = (f32[3,512,96]{1,2,0:T(8,128)}, f32[3,512,96]{1,2,0:T(8,128)S(1)}, u32[]{:S(2)}) copy-start(f32[3,512,96]{1,2,0:T(8,128)S(1)} %get-tuple-element.46) | copy-start | bytes 1769476
  196.5 8.1 copy-start.11
  204.6 2.0 copy-start.8
  204.6 2.3 copy-start.14
  206.9 2.3 copy-start.20
  209.2 2.6 copy-start.17
  211.8 4.5 copy-start.1
  211.8 4.5 copy-start.18
  216.3 4.3 copy-start.30
  225.2 5.9 copy-start.23
  231.1 84.1 %copy-start = (bf16[384,1536]{1,0:T(8,128)(2,1)S(1)}, bf16[384,1536]{1,0:T(8,128)(2,1)}, u32[]{:S(2)}) copy-start(bf16[384,1536]{1,0:T(8,128)(2,1)} %param.10) | copy-start | bytes 3538948
  231.2 118.5 %all-gather.20.cloned.1.call-start = ((), (), s32[]{:S(2)}) async-start(), calls=%async_computation.15 | async-start | bytes 3538944 | tf_op jit(solution)/shard_map/all_gather | solution.py:99
  231.8 209.4 %all-gather.16.cloned.1.call-start = ((), (), s32[]{:S(2)}) async-start(), calls=%async_computation.13 | async-start | bytes 5898240 | tf_op jit(solution)/shard_map/all_gather | solution.py:75
  315.2 1.9 copy-start.2
  317.1 395.1 %copy-start.28 = (f32[384]{0:T(512)}, f32[384]{0:T(512)S(1)}, u32[]{:S(2)}) copy-start(f32[384]{0:T(512)S(1)} %get-tuple-element.37) | copy-start | bytes 4612
  317.1 395.1 %copy-start.32 = (f32[384]{0:T(512)}, f32[384]{0:T(512)S(1)}, u32[]{:S(2)}) copy-start(f32[384]{0:T(512)S(1)} %get-tuple-element.36) | copy-start | bytes 4612
  318.6 155.1 %all-gather.18.cloned.1.call-start = ((), (), s32[]{:S(2)}) async-start(), calls=%async_computation.14 | async-start | bytes 3538944 | tf_op jit(solution)/shard_map/all_gather | solution.py:98
  319.3 188.4 %all-gather.22.cloned.1.call-start = ((), (), s32[]{:S(2)}) async-start(), calls=%async_computation.16 | async-start | bytes 3538944 | tf_op jit(solution)/shard_map/all_gather | solution.py:105
  320.1 278.7 %all-gather.24.cloned.1.call-start = ((), (), s32[]{:S(2)}) async-start(), calls=%async_computation.18 | async-start | bytes 5898240 | tf_op jit(solution)/shard_map/all_gather | solution.py:75
  320.8 388.5 %reduce-scatter.14.cloned.1.call-start = ((), (), s32[]{:S(2)}) async-start(), calls=%async_computation.19 | async-start | bytes 5898240 | tf_op jit(solution)/shard_map/reduce_scatter | solution.py:79
  598.7 14.1 %copy-start.35 = (bf16[1536,1024]{1,0:T(8,128)(2,1)S(1)}, bf16[1536,1024]{1,0:T(8,128)(2,1)}, u32[]{:S(2)}) copy-start(bf16[1536,1024]{1,0:T(8,128)(2,1)} %all-gather.18.cloned.1.call-done) | copy-start | bytes 9437188
  612.8 5.2 copy-start.37
  612.8 5.2 copy-start.38
  612.8 5.2 copy-start.34
  625.4 87.3 %copy-start.5 = (bf16[384,1536]{1,0:T(8,128)(2,1)S(1)}, bf16[384,1536]{1,0:T(8,128)(2,1)}, u32[]{:S(2)}) copy-start(bf16[384,1536]{1,0:T(8,128)(2,1)} %param.11) | copy-start | bytes 3538948
  625.5 179.3 %all-gather.26.cloned.1.call-start = ((), (), s32[]{:S(2)}) async-start(), calls=%async_computation.20 | async-start | bytes 5898240 | tf_op jit(solution)/shard_map/all_gather | solution.py:167
  709.3 3.4 copy-start.7
  712.1 0.6 copy-start.33
  714.7 226.7 %reduce-scatter.26.cloned.1.call-start = ((), (), s32[]{:S(2)}) async-start(), calls=%async_computation.26 | async-start | bytes 3538944 | tf_op jit(solution)/shard_map/reduce_scatter | solution.py:232
  724.1 219.3 %reduce-scatter.24.cloned.1.call-start = ((), (), s32[]{:S(2)}) async-start(), calls=%async_computation.25 | async-start | bytes 3538944 | tf_op jit(solution)/shard_map/reduce_scatter | solution.py:221
  733.9 217.4 %reduce-scatter.22.cloned.1.call-start = ((), (), s32[]{:S(2)}) async-start(), calls=%async_computation.24 | async-start | bytes 3538944 | tf_op jit(solution)/shard_map/reduce_scatter | solution.py:218
  743.4 61.4 %copy-start.36 = (bf16[384,1536]{0,1:T(8,128)(2,1)S(1)}, bf16[384,1536]{0,1:T(8,128)(2,1)}, u32[]{:S(2)}) copy-start(bf16[384,1536]{0,1:T(8,128)(2,1)} %all-gather.14.cloned.1.call-done) | copy-start | bytes 3538948
  743.4 247.7 %reduce-scatter.20.cloned.1.call-start = ((), (), s32[]{:S(2)}) async-start(), calls=%async_computation.23 | async-start | bytes 1327104 | tf_op jit(solution)/shard_map/reduce_scatter | solution.py:229
  810.7 11.0 copy-start.19
  821.7 7.9 copy-start.12
  829.5 23.5 %copy-start.21 = (bf16[3,512,2,96,1]{1,3,4,2,0:T(8,128)(2,1)S(1)}, bf16[3,512,2,96,1]{1,3,4,2,0:T(8,128)(2,1)}, u32[]{:S(2)}) copy-start(bf16[3,512,2,96,1]{1,3,4,2,0:T(8,128)(2,1)} %copy-done.20) | copy-start | bytes 1769476
  878.2 3.6 copy-start.24
  881.8 6.5 copy-start.4
  881.8 6.5 copy-start.22
  888.0 148.7 %reduce-scatter.18.cloned.1.call-start = ((), (), s32[]{:S(2)}) async-start(), calls=%async_computation.22 | async-start | bytes 2654208 | tf_op jit(solution)/shard_map/reduce_scatter | solution.py:215
  888.2 2.0 copy-start.15
  888.2 2.2 copy-start.16
  890.5 2.5 copy-start.10
  890.5 2.5 copy-start.13
  890.5 2.5 copy-start.31
  922.6 201.5 %reduce-scatter.16.cloned.1.call-start = ((), (), s32[]{:S(2)}) async-start(), calls=%async_computation.21 | async-start | bytes 5898240 | tf_op jit(solution)/shard_map/reduce_scatter | solution.py:79
  931.2 281.3 %reduce-scatter.12.cloned.1.call-start = ((), (), s32[]{:S(2)}) async-start(), calls=%async_computation.17 | async-start | bytes 5898240 | tf_op jit(solution)/shard_map/reduce_scatter | solution.py:79
  940.7 183.4 %copy-start.26 = (f32[1536]{0:T(1024)S(1)}, f32[1536]{0:T(1024)}, u32[]{:S(2)}) copy-start(f32[1536]{0:T(1024)} %copy-done.25) | copy-start | bytes 18436
  943.4 269.1 %copy-start.6 = (bf16[384,1536]{1,0:T(8,128)(2,1)S(1)}, bf16[384,1536]{1,0:T(8,128)(2,1)}, u32[]{:S(2)}) copy-start(bf16[384,1536]{1,0:T(8,128)(2,1)} %param.11) | copy-start | bytes 3538948
Sparse Core Ops, SparseCore 0:
  9.9 31.7 all-gather.11
  43.8 89.4 all-gather.9
  135.2 22.3 all-gather.13
  231.3 83.8 reduce-scatter.9
  317.0 32.7 all-gather.19
  351.7 89.3 all-gather.15
  443.0 30.5 all-gather.17
  475.5 32.1 all-gather.21
  509.3 89.3 all-gather.23
  625.6 83.6 reduce-scatter.13
  714.8 89.8 all-gather.25
  808.0 44.5 reduce-scatter.25
  855.9 45.9 reduce-scatter.23
  905.2 46.0 reduce-scatter.21
  954.4 36.6 reduce-scatter.19
  994.3 42.3 reduce-scatter.17
  1038.8 85.2 reduce-scatter.15
  1126.3 86.1 reduce-scatter.11
where the time goes:
time: 1230 us; the launch traced here: 1220 us
  waiting for transfers between devices  809 us (66%)
  matrix products  196 us (16%)
  local copies, waits for them, and re-layouts  92.6 us (8%)
  other arithmetic  60 us (5%)
  blocking collectives  48.9 us (4%)
  between operations  16.3 us (1%)
    all_gather x3, waiting for transfers between devices, widen(): return lax.all_gather(shard_rows, 'tensor', axis=0, tiled=True)  274 us
    reduce_scatter x3, waiting for transfers between devices, narrow(): lax.psum_scatter(partial_value.astype(jnp.bfloat16), 'tensor', scatter_di...  218 us
    reduce_scatter x1, waiting for transfers between devices, local(): lax.psum_scatter(jnp.dot(attn_flat, out_cols, preferred_element_type=jnp....  83.4 us
    all_gather x1, waiting for transfers between devices, local(): grad_full = lax.all_gather(hidden1_rounded, 'tensor', axis=0, tiled=True)  61.3 us
    reduce_scatter x1, waiting for transfers between devices, local(): lax.psum_scatter(qkv_part.astype(jnp.bfloat16), 'dp', scatter_dimension=0...  43.9 us
    reduce_scatter x1, waiting for transfers between devices, local(): lax.psum_scatter(out_part.astype(jnp.bfloat16), 'dp', scatter_dimension=1...  37.9 us
    unnamed x2, blocking collectives  29 us
    unnamed x88, local copies, waits for them, and re-layouts  28.9 us
  transfers between devices with their start and end apart: 18, of which 15 were waited for; matrix products, arithmetic and copies ran while one was open for 25% of the time, Pallas kernels for 0%

commit v1 on v0

--- a/solution.py
+++ b/solution.py
@@ -1,6 +1,8 @@
 import jax
 import jax.numpy as jnp
 from jax import lax
+from jax.experimental import pallas as pl
+from jax.experimental.pallas import tpu as pltpu
 from jax.sharding import PartitionSpec as P
 
 QUERY_HEADS = 16
@@ -246,6 +248,485 @@
     )
 
 
+GROUP = 4
+WINDOW = 256
+LANES = 384
+TILE = 128
+
+
+def kernel_qkv(tokens, weight, cos, sin_up, sin_down, out):
+    product = lax.dot_general(
+        tokens[0], weight[...], (((1,), (1,)), ((), ())), preferred_element_type=jnp.float32
+    )
+    repeat = product.shape[1] // LANES
+    half = HEAD_SIZE // 2
+    c = jnp.concatenate([cos[0]] * repeat, axis=1)
+    u = jnp.concatenate([sin_up[0]] * repeat, axis=1)
+    d = jnp.concatenate([sin_down[0]] * repeat, axis=1)
+    width = product.shape[1]
+    turned = pltpu.roll(product, half, 1) * u + pltpu.roll(product, width - half, 1) * d
+    out[0] = (product * c + turned).astype(out.dtype)
+
+
+def project(tokens, weight, tables):
+    blocks, rows, width = tokens.shape
+    units = weight.shape[0]
+    table_spec = pl.BlockSpec((1, rows, LANES), lambda i: (i, 0, 0))
+    return pl.pallas_call(
+        kernel_qkv,
+        grid=(blocks,),
+        in_specs=[
+            pl.BlockSpec((1, rows, width), lambda i: (i, 0, 0)),
+            pl.BlockSpec((units, width), lambda i: (0, 0)),
+            table_spec,
+            table_spec,
+            table_spec,
+        ],
+        out_specs=pl.BlockSpec((1, rows, units), lambda i: (i, 0, 0)),
+        out_shape=jax.ShapeDtypeStruct((blocks, rows, units), jnp.bfloat16),
+        name="project",
+    )(tokens, weight, *tables)
+
+
+def load_group(core, keep, recv, halo, queries, keyvals):
+    mine, other = keep[0], recv[0]
+    first = core == 0
+    queries[...] = jnp.where(first, mine, other)
+    keyvals[:WINDOW] = halo[0]
+    keyvals[WINDOW:] = jnp.where(first, other, mine)
+
+
+def allowed_tile(lowest, start):
+    low = lowest[0, pl.ds(start, TILE), :]
+    key = lax.broadcasted_iota(jnp.int32, (TILE, TILE + WINDOW), 1)
+    query = lax.broadcasted_iota(jnp.int32, (TILE, TILE + WINDOW), 0)
+    return (key >= low) & (key <= query + WINDOW)
+
+
+def kernel_attend(core_ref, keep, recv, halo, lowest, out, log_out, queries, keyvals):
+    core = core_ref[0]
+    load_group(core, keep, recv, halo, queries, keyvals)
+    heads = queries.shape[1] // HEAD_SIZE
+    repeat = QUERY_HEADS // KEY_VALUE_HEADS
+
+    def body(tile, carry):
+        start = pl.multiple_of(tile * TILE, TILE)
+        allowed = allowed_tile(lowest, start)
+        for head in range(heads):
+            group, r = head // repeat, head % repeat
+            base = group * 2 * HEAD_SIZE
+            q = queries[pl.ds(start, TILE), head * HEAD_SIZE : (head + 1) * HEAD_SIZE]
+            k = keyvals[pl.ds(start, TILE + WINDOW), base : base + HEAD_SIZE]
+            v = keyvals[pl.ds(start, TILE + WINDOW), base + HEAD_SIZE : base + 2 * HEAD_SIZE]
+            s = lax.dot_general(
+                q, k, (((1,), (1,)), ((), ())), preferred_element_type=jnp.float32
+            ) * HEAD_SIZE ** (-0.5)
+            s = jnp.where(allowed, s, NEG_FILL)
+            highest = jnp.max(s, axis=1, keepdims=True)
+            total = highest + jnp.log(jnp.sum(jnp.exp(s - highest), axis=1, keepdims=True))
+            p = jnp.exp(s - total).astype(jnp.bfloat16)
+            o = jnp.dot(p, v, preferred_element_type=jnp.float32).astype(jnp.bfloat16)
+            slot = jnp.where(core == r, 0, 1)
+            out[slot, 0, pl.ds(start, TILE), group * HEAD_SIZE : (group + 1) * HEAD_SIZE] = o
+            log_out[0, pl.ds(start, TILE), head : head + 1] = total
+        return carry
+
+    lax.fori_loop(0, queries.shape[0] // TILE, body, 0)
+
+
+def attend(core, keep, recv, halo, lowest):
+    pairs, rows, units = keep.shape
+    heads = units // HEAD_SIZE
+    spec = pl.BlockSpec((1, rows, units), lambda i: (i, 0, 0))
+    return pl.pallas_call(
+        kernel_attend,
+        grid=(pairs,),
+        in_specs=[
+            pl.BlockSpec(memory_space=pltpu.SMEM),
+            spec,
+            spec,
+            pl.BlockSpec((1, WINDOW, units), lambda i: (i, 0, 0)),
+            pl.BlockSpec((1, rows, 1), lambda i: (i, 0, 0)),
+        ],
+        out_specs=[
+            pl.BlockSpec((2, 1, rows, units // 2), lambda i: (0, i, 0, 0)),
+            pl.BlockSpec((1, rows, heads), lambda i: (i, 0, 0)),
+        ],
+        out_shape=[
+            jax.ShapeDtypeStruct((2, pairs, rows, units // 2), jnp.bfloat16),
+            jax.ShapeDtypeStruct((pairs, rows, heads), jnp.float32),
+        ],
+        scratch_shapes=[
+            pltpu.VMEM((rows, units), jnp.bfloat16),
+            pltpu.VMEM((rows + WINDOW, units), jnp.bfloat16),
+        ],
+        name="attend",
+    )(core, keep, recv, halo, lowest)
+
+
+def turn_back(gradient, cos, sin_up, sin_down):
+    repeat = gradient.shape[1] // LANES
+    half = HEAD_SIZE // 2
+    c = jnp.concatenate([cos] * repeat, axis=1)
+    u = jnp.concatenate([sin_up] * repeat, axis=1)
+    d = jnp.concatenate([sin_down] * repeat, axis=1)
+    width = gradient.shape[1]
+    turned = pltpu.roll(gradient, half, 1) * u + pltpu.roll(gradient, width - half, 1) * d
+    return gradient * c - turned
+
+
+def kernel_attend_back(
+    core_ref, keep, recv, halo, lowest, log_total, grads, grads_other, cos, sin_up, sin_down,
+    query_out, key_out, halo_out, queries, keyvals, totals, query_total,
+):
+    core = core_ref[0]
+    load_group(core, keep, recv, halo, queries, keyvals)
+    totals[...] = jnp.zeros_like(totals)
+    heads = queries.shape[1] // HEAD_SIZE
+    repeat = QUERY_HEADS // KEY_VALUE_HEADS
+    scale = HEAD_SIZE ** (-0.5)
+
+    def body(tile, carry):
+        start = pl.multiple_of(tile * TILE, TILE)
+        allowed = allowed_tile(lowest, start)
+        mine = grads[0, pl.ds(start, TILE), :]
+        other = grads_other[0, pl.ds(start, TILE), :]
+        first = core == 0
+        by_repeat = (jnp.where(first, mine, other), jnp.where(first, other, mine))
+        for group in range(heads // repeat):
+            base = group * 2 * HEAD_SIZE
+            k = keyvals[pl.ds(start, TILE + WINDOW), base : base + HEAD_SIZE]
+            v = keyvals[pl.ds(start, TILE + WINDOW), base + HEAD_SIZE : base + 2 * HEAD_SIZE]
+            key_sum = None
+            for r in range(repeat):
+                head = group * repeat + r
+                q = queries[pl.ds(start, TILE), head * HEAD_SIZE : (head + 1) * HEAD_SIZE]
+                g = by_repeat[r][:, group * HEAD_SIZE : (group + 1) * HEAD_SIZE]
+                s = lax.dot_general(
+                    q, k, (((1,), (1,)), ((), ())), preferred_element_type=jnp.float32
+                ) * scale
+                total = log_total[0, pl.ds(start, TILE), head : head + 1]
+                p = jnp.exp(jnp.where(allowed, s, NEG_FILL) - total)
+                pg = lax.dot_general(
+                    g, v, (((1,), (1,)), ((), ())), preferred_element_type=jnp.float32
+                )
+                inner = jnp.sum(p * pg, axis=1, keepdims=True)
+                sg = (p * (pg - inner) * scale).astype(jnp.bfloat16)
+                query_total[:, head * HEAD_SIZE : (head + 1) * HEAD_SIZE] = jnp.dot(
+                    sg, k, preferred_element_type=jnp.float32
+                )
+                dk = lax.dot_general(
+                    sg, q, (((0,), (0,)), ((), ())), preferred_element_type=jnp.float32
+                )
+                dv = lax.dot_general(
+                    p.astype(jnp.bfloat16), g, (((0,), (0,)), ((), ())),
+                    preferred_element_type=jnp.float32,
+                )
+                both = jnp.concatenate([dk, dv], axis=1)
+                key_sum = both if key_sum is None else key_sum + both
+            totals[pl.ds(start, TILE + WINDOW), base : base + 2 * HEAD_SIZE] += key_sum
+        rows = pl.ds(start, TILE)
+        query_out[0, rows, :] = turn_back(
+            query_total[...], cos[0, rows, :], sin_up[0, rows, :], sin_down[0, rows, :]
+        ).astype(jnp.bfloat16)
+        return carry
+
+    lax.fori_loop(0, queries.shape[0] // TILE, body, 0)
+    key_out[0] = totals[WINDOW:]
+    halo_out[0] = totals[:WINDOW].astype(jnp.bfloat16)
+
+
+def attend_back(core, keep, recv, halo, lowest, log_total, grads, grads_other, tables):
+    pairs, rows, units = keep.shape
+    heads = units // HEAD_SIZE
+    spec = pl.BlockSpec((1, rows, units), lambda i: (i, 0, 0))
+    half_spec = pl.BlockSpec((1, rows, units // 2), lambda i: (i, 0, 0))
+    halo_spec = pl.BlockSpec((1, WINDOW, units), lambda i: (i, 0, 0))
+    table_spec = pl.BlockSpec((1, rows, LANES), lambda i: (i, 0, 0))
+    return pl.pallas_call(
+        kernel_attend_back,
+        grid=(pairs,),
+        in_specs=[
+            pl.BlockSpec(memory_space=pltpu.SMEM),
+            spec,
+            spec,
+            halo_spec,
+            pl.BlockSpec((1, rows, 1), lambda i: (i, 0, 0)),
+            pl.BlockSpec((1, rows, heads), lambda i: (i, 0, 0)),
+            half_spec,
+            half_spec,
+            table_spec,
+            table_spec,
+            table_spec,
+        ],
+        out_specs=[spec, spec, halo_spec],
+        out_shape=[
+            jax.ShapeDtypeStruct((pairs, rows, units), jnp.bfloat16),
+            jax.ShapeDtypeStruct((pairs, rows, units), jnp.float32),
+            jax.ShapeDtypeStruct((pairs, WINDOW, units), jnp.bfloat16),
+        ],
+        scratch_shapes=[
+            pltpu.VMEM((rows, units), jnp.bfloat16),
+            pltpu.VMEM((rows + WINDOW, units), jnp.bfloat16),
+            pltpu.VMEM((rows + WINDOW, units), jnp.float32),
+            pltpu.VMEM((TILE, units), jnp.float32),
+        ],
+        name="attend_back",
+    )(core, keep, recv, halo, lowest, log_total, grads, grads_other, *tables)
+
+
+def kernel_finish_keys(key_sum, halo, cos, sin_up, sin_down, out):
+    rows = key_sum.shape[1]
+    full = key_sum[0]
+    tail = full[rows - WINDOW :] + halo[0].astype(jnp.float32)
+    full = jnp.concatenate([full[: rows - WINDOW], tail], axis=0)
+    out[0] = turn_back(full, cos[0], sin_up[0], sin_down[0]).astype(jnp.bfloat16)
+
+
+def finish_keys(key_sum, halo, tables):
+    pairs, rows, units = key_sum.shape
+    spec = pl.BlockSpec((1, rows, units), lambda i: (i, 0, 0))
+    table_spec = pl.BlockSpec((1, rows, LANES), lambda i: (i, 0, 0))
+    return pl.pallas_call(
+        kernel_finish_keys,
+        grid=(pairs,),
+        in_specs=[
+            spec,
+            pl.BlockSpec((1, WINDOW, units), lambda i: (i, 0, 0)),
+            table_spec,
+            table_spec,
+            table_spec,
+        ],
+        out_specs=spec,
+        out_shape=jax.ShapeDtypeStruct((pairs, rows, units), jnp.bfloat16),
+        name="finish_keys",
+    )(key_sum, halo, *tables)
+
+
+def fast_local(
+    n_dp,
+    n_tensor,
+    block_in,
+    cotangent,
+    segment_ids,
+    attn_gain,
+    qkv_weight,
+    out_weight,
+    mlp_gain,
+    gate_weight,
+    up_weight,
+    down_weight,
+):
+    bf16, f32 = jnp.bfloat16, jnp.float32
+    d_at = lax.axis_index("dp")
+    z_at = lax.axis_index("tensor")
+    core = d_at % 2
+    member = d_at % GROUP
+    upper = d_at // GROUP
+    rows, width = block_in.shape
+    seqs, length = segment_ids.shape
+    half = width // 2
+
+    def swap(value, bit):
+        return lax.ppermute(value, "dp", [(i, i ^ bit) for i in range(n_dp)])
+
+    def own_order(value):
+        turned = jnp.concatenate([value[..., half:], value[..., :half]], axis=-1)
+        return jnp.where(upper == 0, value, turned)
+
+    shards = [qkv_weight.T, out_weight, gate_weight.T, up_weight.T, down_weight]
+    quarters = [s.reshape(GROUP, s.shape[0] // GROUP, s.shape[1]) for s in shards]
+    sizes = [q.shape[1] for q in quarters]
+
+    def deal(parcel):
+        pieces = [lax.dynamic_index_in_dim(parcel, member, 0, keepdims=False)]
+        for k in range(1, GROUP):
+            sent = lax.dynamic_index_in_dim(parcel, member ^ k, 0, keepdims=False)
+            pieces.append(swap(sent, k))
+        stacked = jnp.stack(pieces)
+        ordered = [
+            lax.dynamic_index_in_dim(stacked, member ^ i, 0, keepdims=False) for i in range(GROUP)
+        ]
+        return jnp.concatenate(ordered, axis=-1)
+
+    def spread(piece):
+        mine = lax.all_gather(piece, "tensor", axis=0, tiled=True)
+        return jnp.concatenate([mine, swap(mine, GROUP)], axis=1)
+
+    first_deal = deal(quarters[0])
+    rest_deal = deal(jnp.concatenate(quarters[1:], axis=1))
+    offsets = [0]
+    for size in sizes[1:]:
+        offsets.append(offsets[-1] + size)
+    dealt = [first_deal] + [
+        rest_deal[offsets[i] : offsets[i + 1]] for i in range(len(sizes) - 1)
+    ]
+    qkv_full, out_full, gate_full, up_full, down_full = [spread(piece) for piece in dealt]
+
+    def gather_pair(value):
+        return jnp.stack([value, swap(value, 2)])
+
+    def gather(value):
+        pair = gather_pair(value)
+        return jnp.concatenate([pair, swap(pair, 1)], axis=0)
+
+    def scatter(partial_value):
+        blocks = partial_value.reshape(GROUP, rows, partial_value.shape[-1])
+        got = swap(blocks[2:].astype(bf16), 1)
+        pair = blocks[:2].astype(f32) + got.astype(f32)
+        return pair[0] + swap(pair[1].astype(bf16), 2).astype(f32)
+
+    starts_row = jnp.arange(length, dtype=jnp.int32)[None, :] - doc_positions(segment_ids)
+    stream = starts_row + jnp.arange(seqs, dtype=jnp.int32)[:, None] * length
+    stream = stream.reshape(n_tensor, rows)
+    first_key = lax.dynamic_index_in_dim(stream, z_at, 0, keepdims=False)
+    own_position = z_at * rows + jnp.arange(rows, dtype=jnp.int32) - first_key
+    small = jnp.concatenate(
+        [attn_gain.astype(f32), mlp_gain.astype(f32), own_position.astype(f32), first_key.astype(f32)]
+    )
+    smalls = lax.all_gather(small, "dp", axis=0)
+    part = attn_gain.shape[0]
+    gain_attn = own_order(smalls[:, :part].reshape(width))
+    gain_mlp = own_order(smalls[:, part : 2 * part].reshape(width))
+    block_order = jnp.stack([d_at, d_at ^ 2, d_at ^ 1, d_at ^ 3])
+    token_info = smalls[:, 2 * part :][block_order]
+    positions = token_info[:, :rows]
+    lowest = token_info[:2, rows:].astype(jnp.int32) - z_at * rows + WINDOW
+    tile_at = jnp.arange(rows, dtype=jnp.int32) // TILE * TILE
+    lowest = (lowest - tile_at[None, :])[:, :, None]
+
+    lane = jnp.arange(LANES, dtype=jnp.int32)
+    within = lane % HEAD_SIZE
+    frequency = jnp.power(
+        ROPE_BASE, -(2.0 * (within % (HEAD_SIZE // 2)).astype(f32)) / HEAD_SIZE
+    )
+    angles = positions[:, :, None] * frequency
+    cosine, sine = jnp.cos(angles), jnp.sin(angles)
+    is_key = (lane % (2 * HEAD_SIZE)) < HEAD_SIZE
+    is_second = within >= HEAD_SIZE // 2
+
+    def tables_for(turns, count):
+        return (
+            jnp.where(turns, cosine[:count], 1.0),
+            jnp.where(turns & is_second, sine[:count], 0.0),
+            jnp.where(turns & ~is_second, -sine[:count], 0.0),
+        )
+
+    whole_lane = jnp.full((LANES,), True)
+    query_tables = tables_for(whole_lane, 2)
+    key_tables = tables_for(is_key, 2)
+    own_tables = tables_for(is_key | (core == 0), GROUP)
+
+    residual = own_order(block_in).astype(f32)
+    cot_own = own_order(cotangent)
+    scale_attn = rms_scale(residual)
+    normed1 = gather((residual * scale_attn * gain_attn).astype(bf16))
+    grad_rows = gather(cot_own)
+
+    projected = project(normed1, qkv_full, own_tables)
+    keep, send = projected[:2], projected[2:]
+    recv = swap(send, 1)
+    tail = jnp.where(core == 0, recv[:, rows - WINDOW :], keep[:, rows - WINDOW :])
+    halo = lax.ppermute(tail, "tensor", [(i, i + 1) for i in range(n_tensor - 1)])
+    core_arg = core.astype(jnp.int32).reshape(1)
+    outs, log_total = attend(core_arg, keep, recv, halo, lowest)
+    attended = jnp.concatenate([outs[0], swap(outs[1], 1)], axis=0)
+    attn_flat = attended.reshape(GROUP * rows, attended.shape[-1])
+    hidden1 = residual + scatter(
+        jnp.dot(attn_flat, out_full, preferred_element_type=f32).astype(bf16)
+    )
+    scale_mlp = rms_scale(hidden1)
+    normed2 = gather((hidden1 * scale_mlp * gain_mlp).astype(bf16)).reshape(GROUP * rows, width)
+    grad_rows = grad_rows.reshape(GROUP * rows, width)
+
+    def to_units(tokens, weight):
+        return jnp.einsum("td,ud->tu", tokens, weight, preferred_element_type=f32)
+
+    def grad_of(left, right):
+        return jnp.einsum("tu,td->ud", left, right, preferred_element_type=f32).astype(bf16)
+
+    gate = to_units(normed2, gate_full)
+    up_value = to_units(normed2, up_full)
+    sigmoid_gate = jax.nn.sigmoid(gate)
+    activated = (gate * sigmoid_gate * up_value).astype(bf16)
+    act_grad = to_units(grad_rows, down_full)
+    gate_delta = (act_grad * up_value * sigmoid_gate * (1.0 + gate * (1.0 - sigmoid_gate))).astype(
+        bf16
+    )
+    up_delta = (act_grad * gate * sigmoid_gate).astype(bf16)
+    normed2_term = jnp.dot(gate_delta, gate_full, preferred_element_type=f32) + jnp.dot(
+        up_delta, up_full, preferred_element_type=f32
+    )
+    normed2_grad = scatter(normed2_term.astype(bf16))
+    mlp_delta = scatter(jnp.dot(activated, down_full, preferred_element_type=f32).astype(bf16))
+    block_out = own_order((hidden1 + mlp_delta).astype(bf16))
+    down_part = grad_of(activated, grad_rows)
+    gate_part = grad_of(gate_delta, normed2)
+    up_part = grad_of(up_delta, normed2)
+    mlp_gain_part = jnp.sum(normed2_grad * hidden1 * scale_mlp, axis=0)
+    hidden1_grad = cot_own.astype(f32) + norm_back(hidden1, scale_mlp, gain_mlp, normed2_grad)
+    grad_full = gather(hidden1_grad.astype(bf16)).reshape(GROUP * rows, width)
+    attended_grad = to_units(grad_full, out_full).astype(bf16)
+    out_part = grad_of(attn_flat, grad_full)
+    attended_grad = attended_grad.reshape(GROUP, rows, attended_grad.shape[-1])
+    grads_other = swap(attended_grad[2:], 1)
+    query_grad, key_sum, halo_grad = attend_back(
+        core_arg, keep, recv, halo, lowest, log_total, attended_grad[:2], grads_other, query_tables
+    )
+    halo_back = lax.ppermute(halo_grad, "tensor", [(i + 1, i) for i in range(n_tensor - 1)])
+    key_grad = finish_keys(key_sum, halo_back, key_tables)
+    kept = jnp.where(core == 0, query_grad, key_grad)
+    passed = jnp.where(core == 0, key_grad, query_grad)
+    projected_grad = jnp.concatenate([kept, swap(passed, 1)], axis=0)
+    projected_grad = projected_grad.reshape(GROUP * rows, projected_grad.shape[-1])
+    normed1_flat = normed1.reshape(GROUP * rows, width)
+    normed1_grad = scatter(
+        jnp.dot(projected_grad, qkv_full, preferred_element_type=f32).astype(bf16)
+    )
+    qkv_part = grad_of(projected_grad, normed1_flat)
+    attn_gain_part = jnp.sum(normed1_grad * residual * scale_attn, axis=0)
+    input_grad = own_order(
+        (hidden1_grad + norm_back(residual, scale_attn, gain_attn, normed1_grad)).astype(bf16)
+    )
+
+    def collect(part_grad):
+        summed = part_grad[:, :half].astype(f32) + swap(part_grad[:, half:], GROUP).astype(f32)
+        piece = lax.psum_scatter(
+            summed.astype(bf16), "tensor", scatter_dimension=0, tiled=True
+        )
+        units = piece.shape[0]
+        columns = piece.reshape(units, GROUP, half // GROUP).transpose(1, 0, 2)
+        pieces = [lax.dynamic_index_in_dim(columns, member, 0, keepdims=False)]
+        for k in range(1, GROUP):
+            sent = lax.dynamic_index_in_dim(columns, member ^ k, 0, keepdims=False)
+            pieces.append(swap(sent, k))
+        stacked = jnp.stack(pieces)
+        ordered = [
+            lax.dynamic_index_in_dim(stacked, member ^ i, 0, keepdims=False) for i in range(GROUP)
+        ]
+        return jnp.concatenate(ordered, axis=0)
+
+    down_grad = collect(down_part).astype(f32)
+    gate_grad = collect(gate_part).T.astype(f32)
+    up_grad = collect(up_part).T.astype(f32)
+    out_grad = collect(out_part).astype(f32)
+    qkv_grad = collect(qkv_part).T.astype(f32)
+    gains = own_order(jnp.stack([attn_gain_part, mlp_gain_part]))
+    gains = lax.psum(gains, ("dp", "tensor"))
+    gains = lax.dynamic_slice_in_dim(gains, d_at * part, part, axis=1)
+    return (
+        block_out,
+        input_grad,
+        gains[0],
+        qkv_grad,
+        out_grad,
+        gains[1],
+        gate_grad,
+        up_grad,
+        down_grad,
+    )
+
+
 def solution(mesh):
     in_specs = (
         P(("dp", "tensor"), None),
@@ -270,4 +751,13 @@
         P("dp", "tensor"),
         P("tensor", "dp"),
     )
-    return jax.shard_map(local, mesh=mesh, in_specs=in_specs, out_specs=out_specs, check_vma=False)
+    n_dp, n_tensor = mesh.shape["dp"], mesh.shape["tensor"]
+
+    def body(*arrays):
+        rows = arrays[0].shape[0]
+        groups = arrays[4].shape[1] // (4 * HEAD_SIZE)
+        if n_dp == 2 * GROUP and groups == 2 and rows >= WINDOW and rows % TILE == 0:
+            return fast_local(n_dp, n_tensor, *arrays)
+        return local(*arrays)
+
+    return jax.shard_map(body, mesh=mesh, in_specs=in_specs, out_specs=out_specs, check_vma=False)

time: 1230 us -> 841 us (0.68)
  waiting for transfers between devices: 809 us -> 348 us
  matrix products: 196 us -> 91.9 us
  Pallas kernels: 0 us -> 66 us
  other arithmetic: 60 us -> 98.4 us
  starting transfers between devices: 1.11 us -> 39.1 us
  blocking collectives: 48.9 us -> 80.1 us
    reduce_scatter x9 -> x5, waiting for transfers between devices: 389 us -> 2.39 us  [collect(): lax.psum_scatter(summed.astype(bf16), 'tensor', scatter_dimension=0, tile...]
    all_gather x9 -> x4, waiting for transfers between devices: 415 us -> 59.6 us  [spread(): mine = lax.all_gather(piece, 'tensor', axis=0, tiled=True)]
    ppermute x0 -> x53, waiting for transfers between devices: none -> 286 us  [the longest x51 266 us: swap(): return lax.ppermute(value, 'dp', [(i, i ^ bit) for i in range(n_dp)])]
    dot_general x21 -> x14, matrix products: 196 us -> 91.9 us  [the longest x5 33.8 us: grad_of(): jnp.einsum('tu,td->ud', left, right, preferred_element_type=f32)]
    pallas_call x0 -> x4, Pallas kernels: none -> 66 us  [the longest x1 28.4 us: attend_back(): pl.pallas_call(kernel_attend_back, grid=(pairs,), in_specs=[pl.BlockSpec(...]
    all_gather x0 -> x2, blocking collectives: none -> 40 us  [the longest x1 29.4 us: spread(): mine = lax.all_gather(piece, 'tensor', axis=0, tiled=True)]
    ppermute x0 -> x53, starting transfers between devices: none -> 38.2 us  [the longest x51 33.7 us: swap(): return lax.ppermute(value, 'dp', [(i, i ^ bit) for i in range(n_dp)])]
    unnamed x2 -> x0, blocking collectives: 29 us -> none
  transfers between devices with their start and end apart: 18 -> 62, of which waited for: 15 -> 25; matrix products, arithmetic and copies ran while one was open for 25% -> 26% of each run, Pallas kernels for 0% -> 7%
where the time goes in v1:
time: 841 us; the launch traced here: 834 us
  waiting for transfers between devices  348 us (41%)
  other arithmetic  98.4 us (12%)
  local copies, waits for them, and re-layouts  94.4 us (11%)
  matrix products  91.9 us (11%)
  blocking collectives  80.1 us (10%)
  Pallas kernels  66 us (8%)
  starting transfers between devices  39.1 us (5%)
  between operations  15.8 us (2%)
    ppermute x51, waiting for transfers between devices, swap(): return lax.ppermute(value, 'dp', [(i, i ^ bit) for i in range(n_dp)])  266 us
    all_gather x4, waiting for transfers between devices, spread(): mine = lax.all_gather(piece, 'tensor', axis=0, tiled=True)  59.6 us
    psum x1, blocking collectives, fast_local(): gains = lax.psum(gains, ('dp', 'tensor'))  40.1 us
    dot_general x5, matrix products, grad_of(): jnp.einsum('tu,td->ud', left, right, preferred_element_type=f32)  33.8 us
    ppermute x51, starting transfers between devices, swap(): return lax.ppermute(value, 'dp', [(i, i ^ bit) for i in range(n_dp)])  33.7 us
    all_gather x1, blocking collectives, spread(): mine = lax.all_gather(piece, 'tensor', axis=0, tiled=True)  29.4 us
    pallas_call x1, Pallas kernels, attend_back(): pl.pallas_call(kernel_attend_back, grid=(pairs,), in_specs=[pl.BlockSpec(...  28.4 us
    dot_general x4, matrix products, to_units(): return jnp.einsum('td,ud->tu', tokens, weight, preferred_element_type=f32)  28.3 us
  transfers between devices with their start and end apart: 62, of which 25 were waited for; matrix products, arithmetic and copies ran while one was open for 26% of the time, Pallas kernels for 7%

profile of v1, /device:TPU:0, one launch (start us, length us, event | category | flops | bytes accessed | tf_op | source)
XLA Modules:
  0.0 834.2 jit_solution(5020711860747794067)
XLA Ops:
  11.2 10.6 %all-gather.1 = f32[8,1,1152]{2,1,0:T(1,128)S(1)} all-gather(f32[1,1,1152]{2,1,0:T(1,128)S(1)} %reshape.465), channel_id=2, replica_groups=mesh['dp'=8,'tensor'=4] {'dp'}, dimensions={0}, use_global_device_ids=true | all-gather | bytes 41472 | tf_op jit(solution)/shard_map/all_gather | solution.py:587
  32.5 25.8 %collective-permute-done.3 = bf16[192,192]{1,0:T(8,128)(2,1)S(1)} collective-permute-done((bf16[192,192]{1,0:T(8,128)(2,1)S(1)}, bf16[192,192]{1,0:T(8,128)(2,1)S(1)}, u32[]{:S(2)}, u32[]{:S(2)}) %collective-permute-start.3) | collective-permute-done | bytes 73760 | tf_op jit(solution)/shard_map/ppermute | solution.py:531
  72.1 18.9 %all-gather.7.cloned.1.call-done = bf16[768,768]{1,0:T(8,128)(2,1)} async-done(((bf16[192,768]{1,0:T(8,128)(2,1)}), bf16[768,768]{1,0:T(8,128)(2,1)}) %all-gather.7.cloned.1.call-update) | async-done | bytes 1179664 | tf_op jit(solution)/shard_map/all_gather | solution.py:553
  94.7 11.9 %multiply_sine_fusion = (f32[4,384,384]{2,1,0:T(8,128)}, f32[4,384,384]{2,1,0:T(8,128)}, f32[4,384,384]{2,1,0:T(8,128)}, f32[4,384,384]{2,1,0:T(8,128)}, f32[4,384,384]{2,1,0:T(8,128)}) fusion(f32[384]{0:T(512)S(1)} %fusion.34, f32[4,384]{1,0:T(4,128)S(1)} %slice.312, pred[384]{0:T(512)(128)(4,1)S(1)} %get-tuple-element.163, pred[384]{0:T(512)(128)(4,1)S(1)} %fusion.54, ...), kind=kLoop, calls=%fused_computation.27 | loop fusion | flops 2949120 | bytes 11805312 | tf_op jit(solution)/shard_map/sin | solution.py:604
  107.8 10.7 %collective-permute-done.5 = bf16[768,768]{1,0:T(8,128)(2,1)} collective-permute-done((bf16[768,768]{1,0:T(8,128)(2,1)}, bf16[768,768]{1,0:T(8,128)(2,1)}, u32[]{:S(2)}, u32[]{:S(2)}) %collective-permute-start.5) | collective-permute-done | bytes 1179680 | tf_op jit(solution)/shard_map/ppermute | solution.py:531
  118.5 2.4 constant_dynamic-update-slice_fusion.weight
  120.9 3.7 pad_maximum_fusion.tokens
  124.6 10.2 %project.1 = bf16[4,384,768]{2,1,0:T(8,128)(2,1)} custom-call(bf16[4,384,1536]{2,1,0:T(8,128)(2,1)} %pad_maximum_fusion.tokens, bf16[768,1536]{1,0:T(8,128)(2,1)} %constant_dynamic-update-slice_fusion.weight, f32[4,384,384]{2,1,0:T(8,128)} %get-tuple-element.151.cos, f32[4,384,384]{2,1,0:T(8,128)} %get-tuple-element.153.sin_up, ...), custom_call_target="tpu_custom_call" | custom-call | tf_op jit(solution)/shard_map/project/pallas_call | solution.py:275
  134.9 3.3 fusion.60
  140.0 2.8 constant_dynamic-slice_fusion.17
  148.9 6.5 collective-permute-done.10
  157.0 4.0 collective-permute-done.11
  162.5 3.5 pad_maximum_fusion.10
  166.0 2.8 constant_dynamic-slice_fusion.13
  168.9 2.5 slice_select_fusion.2
  171.4 3.3 collective-permute-start.7
  175.9 29.4 %all_gather.24 = bf16[384,768]{1,0:T(8,128)(2,1)} all-gather(bf16[96,768]{1,0:T(8,128)(2,1)S(1)} %copy.76), channel_id=1, replica_groups=mesh['dp'=8,'tensor'=4] {'tensor'}, dimensions={0}, use_global_device_ids=true | all-gather | bytes 737280 | tf_op jit(solution)/shard_map/all_gather | solution.py:553
  207.7 22.5 %attend.1 = (bf16[2,2,384,384]{3,2,1,0:T(8,128)(2,1)}, f32[2,384,8]{2,1,0:T(8,128)}) custom-call(s32[1]{0:T(128)} %bitcast.core_ref, bf16[2,384,768]{2,1,0:T(8,128)(2,1)} %get-tuple-element.68.keep, bf16[2,384,768]{2,1,0:T(8,128)(2,1)} %copy-done.12, bf16[2,256,768]{2,1,0:T(8,128)(2,1)} %copy-done.24, s32[2,384,1]{2,1,0:T(8,128)} %copy.72.lowest), custom_call_target="tpu_custom_call" | custom-call | tf_op jit(solution)/shard_map/attend/pallas_call | solution.py:341
  237.9 2.8 convolution_convert_fusion.2
  240.7 2.5 fusion.59
  248.2 3.1 convert_add_fusion.4
  258.6 16.7 %collective-permute-done.22 = bf16[384,1536]{1,0:T(8,128)(2,1)S(1)} collective-permute-done((bf16[384,1536]{1,0:T(8,128)(2,1)S(1)}, bf16[384,1536]{1,0:T(8,128)(2,1)S(1)}, u32[]{:S(2)}, u32[]{:S(2)}) %collective-permute-start.22) | collective-permute-done | bytes 1179680 | tf_op jit(solution)/shard_map/ppermute | solution.py:531
  277.1 22.6 %collective-permute-done.14 = bf16[384,1536]{1,0:T(8,128)(2,1)} collective-permute-done((bf16[384,1536]{1,0:T(8,128)(2,1)}, bf16[384,1536]{1,0:T(8,128)(2,1)}, u32[]{:S(2)}, u32[]{:S(2)}) %collective-permute-start.14) | collective-permute-done | bytes 1179680 | tf_op jit(solution)/shard_map/ppermute | solution.py:531
  305.0 4.2 all-gather.11.cloned.1.call-done
  310.7 36.4 %all-gather.13.cloned.1.call-done = bf16[1024,768]{0,1:T(8,128)(2,1)} async-done(((bf16[256,768]{0,1:T(8,128)(2,1)}), bf16[1024,768]{0,1:T(8,128)(2,1)}) %all-gather.13.cloned.1.call-update) | async-done | bytes 1572880 | tf_op jit(solution)/shard_map/all_gather | solution.py:553
  358.0 17.7 %collective-permute-done.18 = bf16[1024,768]{0,1:T(8,128)(2,1)} collective-permute-done((bf16[1024,768]{0,1:T(8,128)(2,1)}, bf16[1024,768]{0,1:T(8,128)(2,1)}, u32[]{:S(2)}, u32[]{:S(2)}) %collective-permute-start.18) | collective-permute-done | bytes 1572896 | tf_op jit(solution)/shard_map/ppermute | solution.py:531
  377.2 30.0 %collective-permute-done.19 = bf16[1024,768]{0,1:T(8,128)(2,1)S(1)} collective-permute-done((bf16[1024,768]{0,1:T(8,128)(2,1)}, bf16[1024,768]{0,1:T(8,128)(2,1)S(1)}, u32[]{:S(2)}, u32[]{:S(2)}) %collective-permute-start.19) | collective-permute-done | bytes 1572896 | tf_op jit(solution)/shard_map/ppermute | solution.py:531
  407.4 7.0 fusion.71
  415.0 7.0 fusion.70
  421.9 11.7 %multiply_convert_fusion.1 = (bf16[1536,1024]{1,0:T(8,128)(2,1)S(1)}, bf16[1536,1024]{1,0:T(8,128)(2,1)}, bf16[1536,1024]{1,0:T(8,128)(2,1)S(1)}) fusion(f32[1536,1024]{1,0:T(8,128)} %fusion.71, f32[1536,1024]{1,0:T(8,128)} %fusion.70, bf16[1536,1536]{1,0:T(8,128)(2,1)S(1)} %bitcast.298, bf16[1024,1536]{0,1:T(8,128)(2,1)S(1)} %copy-done.47), kind=kOutput, calls=%fused_computation.6 | convolution fusion | flops 4857004032 | bytes 29884416 | tf_op jit(solution)/shard_map/td,ud->tu/dot_general | solution.py:643
  433.6 9.6 %convolution_convert_fusion.3 = bf16[1024,1536]{1,0:T(8,128)(2,1)S(1)} fusion(bf16[1536,1024]{1,0:T(8,128)(2,1)} %get-tuple-element.48, bf16[1536,1536]{1,0:T(8,128)(2,1)S(1)} %bitcast.304), kind=kOutput, calls=%fused_computation.24 | convolution fusion | flops 4833411072 | bytes 11010048 | tf_op jit(solution)/shard_map/tu,td->ud/dot_general | solution.py:646
  445.2 8.1 fusion.72
  453.3 7.8 add_convert_fusion
  461.1 2.7 fusion.57
  465.7 5.3 convolution_convert_fusion
  471.0 2.6 fusion.58
  473.6 4.2 collective-permute-done.49
  479.4 3.1 convert_add_fusion.2
  484.2 2.9 convert_add_fusion.3
  487.8 5.6 convolution_convert_fusion.4
  494.1 17.5 %collective-permute-done.25 = bf16[384,1536]{1,0:T(8,128)(2,1)S(1)} collective-permute-done((bf16[384,1536]{1,0:T(8,128)(2,1)S(1)}, bf16[384,1536]{1,0:T(8,128)(2,1)S(1)}, u32[]{:S(2)}, u32[]{:S(2)}) %collective-permute-start.25) | collective-permute-done | bytes 1179680 | tf_op jit(solution)/shard_map/ppermute | solution.py:531
  512.8 20.3 %collective-permute-done.21 = bf16[384,1536]{1,0:T(8,128)(2,1)S(1)} collective-permute-done((bf16[384,1536]{1,0:T(8,128)(2,1)S(1)}, bf16[384,1536]{1,0:T(8,128)(2,1)S(1)}, u32[]{:S(2)}, u32[]{:S(2)}) %collective-permute-start.21) | collective-permute-done | bytes 1179680 | tf_op jit(solution)/shard_map/ppermute | solution.py:531
  533.1 2.9 fusion.55
  538.2 22.2 %collective-permute-done.26 = bf16[384,1536]{1,0:T(8,128)(2,1)S(1)} collective-permute-done((bf16[384,1536]{1,0:T(8,128)(2,1)}, bf16[384,1536]{1,0:T(8,128)(2,1)S(1)}, u32[]{:S(2)}, u32[]{:S(2)}) %collective-permute-start.26) | collective-permute-done | bytes 1179680 | tf_op jit(solution)/shard_map/ppermute | solution.py:531
  562.6 7.8 convolution_convert_fusion.5
  571.7 35.1 %collective-permute-done.41 = bf16[1024,768]{1,0:T(8,128)(2,1)S(1)} collective-permute-done((bf16[1024,768]{1,0:T(8,128)(2,1)S(1)}, bf16[1024,768]{1,0:T(8,128)(2,1)S(1)}, u32[]{:S(2)}, u32[]{:S(2)}) %collective-permute-start.41) | collective-permute-done | bytes 1572896 | tf_op jit(solution)/shard_map/ppermute | solution.py:531
  608.6 2.5 pad_maximum_fusion.3
  611.2 2.6 convolution_convert_fusion.6
  617.3 2.5 negate_select_fusion.1
  620.5 28.4 %attend_back.1 = (bf16[2,384,768]{2,1,0:T(8,128)(2,1)}, f32[2,384,768]{2,1,0:T(8,128)}, bf16[2,256,768]{2,1,0:T(8,128)(2,1)}) custom-call(s32[1]{0:T(128)} %bitcast.core_ref, bf16[2,384,768]{2,1,0:T(8,128)(2,1)} %get-tuple-element.68.keep, bf16[2,384,768]{2,1,0:T(8,128)(2,1)} %copy-done.12, bf16[2,256,768]{2,1,0:T(8,128)(2,1)} %copy-done.24, ...), custom_call_target="tpu_custom_call" | custom-call | tf_op jit(solution)/shard_map/attend_back/pallas_call | solution.py:446
  650.2 19.9 %collective-permute-done.29.halo = bf16[2,256,768]{2,1,0:T(8,128)(2,1)S(1)} collective-permute-done((bf16[2,256,768]{2,1,0:T(8,128)(2,1)}, bf16[2,256,768]{2,1,0:T(8,128)(2,1)S(1)}, u32[]{:S(2)}, u32[]{:S(2)}) %collective-permute-start.29) | collective-permute-done | bytes 786464 | tf_op jit(solution)/shard_map/ppermute | solution.py:676
  670.9 4.8 finish_keys.1
  675.8 2.9 broadcast_select_fusion.2
  690.0 5.7 convolution_convert_fusion.1
  697.8 4.2 fusion
  711.2 7.9 collective-permute-done.37
  720.4 6.6 bitcast_convert_fusion
  737.1 2.4 reduce-scatter.8.cloned.1.call-done
  744.1 18.8 %collective-permute-done.39 = bf16[96,192]{1,0:T(8,128)(2,1)S(1)} collective-permute-done((bf16[96,192]{1,0:T(8,128)(2,1)S(1)}, bf16[96,192]{1,0:T(8,128)(2,1)S(1)}, u32[]{:S(2)}, u32[]{:S(2)}) %collective-permute-start.39) | collective-permute-done | bytes 36896 | tf_op jit(solution)/shard_map/ppermute | solution.py:531
  764.0 2.7 add_convert_fusion.4
  766.7 3.5 fusion.10
  770.9 40.1 %psum.7 = f32[2,1536]{1,0:T(2,128)} all-reduce(f32[2,1536]{1,0:T(2,128)} %fusion.22), channel_id=1, replica_groups=mesh['dp'=8,'tensor'=4] {'dp','tensor'}, use_global_device_ids=true, to_apply=%region_8.9 | all-reduce | flops 3072 | bytes 24576 | tf_op jit(solution)/shard_map/psum | solution.py:715
  811.7 2.8 fusion.7
  818.2 2.3 collective-permute-start.35
  (426 shorter events, 163.2 us)
Async XLA Ops:
  7.2 83.9 %all-gather.7.cloned.1.call-start = ((), (), s32[]{:S(2)}) async-start(), calls=%async_computation.5 | async-start | bytes 1474560 | tf_op jit(solution)/shard_map/all_gather | solution.py:553
  25.2 274.6 %copy-start = (bf16[384,1536]{1,0:T(8,128)(2,1)}, bf16[384,1536]{1,0:T(8,128)(2,1)S(1)}, u32[]{:S(2)}) copy-start(bf16[384,1536]{1,0:T(8,128)(2,1)S(1)} %get-tuple-element.46) | copy-start | bytes 3538948
  27.2 33.5 %collective-permute-start = (bf16[384,1536]{1,0:T(8,128)(2,1)}, bf16[384,1536]{1,0:T(8,128)(2,1)S(1)}, u32[]{:S(2)}, u32[]{:S(2)}) collective-permute-start(bf16[384,1536]{1,0:T(8,128)(2,1)} %fusion.3), channel_id=1, source_target_pairs={{0,8},{4,12},{8,0},{12,4},{16,24},{20,28},{24,16},{28,20},{1,9},{5... | collective-permute-start | bytes 3538952 | tf_op jit(solution)/shard_map/ppermute | solution.py:531
  30.0 2.5 collective-permute-start.2
  30.3 28.0 %collective-permute-start.3 = (bf16[192,192]{1,0:T(8,128)(2,1)S(1)}, bf16[192,192]{1,0:T(8,128)(2,1)S(1)}, u32[]{:S(2)}, u32[]{:S(2)}) collective-permute-start(bf16[192,192]{1,0:T(8,128)(2,1)S(1)} %bitcast.334), channel_id=1, source_target_pairs={{0,8},{4,12},{8,0},{12,4},{16,24},{20,28},{24,16},{28,20},{1,9},{5... | collective-permute-start | bytes 221192 | tf_op jit(solution)/shard_map/ppermute | solution.py:531
  31.1 28.2 %collective-permute-start.4 = (bf16[192,192]{1,0:T(8,128)(2,1)S(1)}, bf16[192,192]{1,0:T(8,128)(2,1)S(1)}, u32[]{:S(2)}, u32[]{:S(2)}) collective-permute-start(bf16[192,192]{1,0:T(8,128)(2,1)S(1)} %bitcast.335), channel_id=1, source_target_pairs={{0,12},{4,8},{8,4},{12,0},{16,28},{20,24},{24,20},{28,16},{1,13},{... | collective-permute-start | bytes 221192 | tf_op jit(solution)/shard_map/ppermute | solution.py:531
  60.3 244.2 %all-gather.9.cloned.1.call-start = ((), (), s32[]{:S(2)}) async-start(), calls=%async_computation.6 | async-start | bytes 1966080 | tf_op jit(solution)/shard_map/all_gather | solution.py:553
  60.7 60.2 %copy-start.8 = (bf16[1,384,1536]{2,1,0:T(8,128)(2,1)}, bf16[1,384,1536]{2,1,0:T(8,128)(2,1)S(1)}, u32[]{:S(2)}) copy-start(bf16[1,384,1536]{2,1,0:T(8,128)(2,1)S(1)} %fusion.98) | copy-start | bytes 3538948
  62.5 58.4 %collective-permute-start.1 = (bf16[2,384,1536]{2,1,0:T(8,128)(2,1)}, bf16[2,384,1536]{2,1,0:T(8,128)(2,1)}, u32[]{:S(2)}, u32[]{:S(2)}) collective-permute-start(bf16[2,384,1536]{2,1,0:T(8,128)(2,1)} %pad_maximum_fusion.4), channel_id=1, source_target_pairs={{0,4},{4,0},{8,12},{12,8},{16,20},{20,16},{24,28},{28,24},{1,5},{5... | collective-permute-start | bytes 7077896 | tf_op jit(solution)/shard_map/ppermute | solution.py:531
  91.1 27.4 %collective-permute-start.5 = (bf16[768,768]{1,0:T(8,128)(2,1)}, bf16[768,768]{1,0:T(8,128)(2,1)}, u32[]{:S(2)}, u32[]{:S(2)}) collective-permute-start(bf16[768,768]{1,0:T(8,128)(2,1)} %all-gather.7.cloned.1.call-done), channel_id=1, source_target_pairs={{0,16},{4,20},{8,24},{12,28},{16,0},{20,4},{24,8},{28,12},{1,17},{... | collective-permute-start | bytes 3538952 | tf_op jit(solution)/shard_map/ppermute | solution.py:531
  138.1 30.7 %collective-permute-start.6 = (bf16[2,384,768]{2,1,0:T(8,128)(2,1)}, bf16[2,384,768]{2,1,0:T(8,128)(2,1)S(1)}, u32[]{:S(2)}, u32[]{:S(2)}) collective-permute-start(bf16[2,384,768]{2,1,0:T(8,128)(2,1)} %get-tuple-element.67), channel_id=1, source_target_pairs={{0,4},{4,0},{8,12},{12,8},{16,20},{20,16},{24,28},{28,24},{1,5},{5... | collective-permute-start | bytes 3538952 | tf_op jit(solution)/shard_map/ppermute | solution.py:531
  142.9 4.5 collective-permute-start.9
  144.2 11.2 %collective-permute-start.10 = (bf16[864,192]{0,1:T(8,128)(2,1)}, bf16[864,192]{0,1:T(8,128)(2,1)}, u32[]{:S(2)}, u32[]{:S(2)}) collective-permute-start(bf16[864,192]{0,1:T(8,128)(2,1)} %bitcast.269), channel_id=1, source_target_pairs={{0,8},{4,12},{8,0},{12,4},{16,24},{20,28},{24,16},{28,20},{1,9},{5... | collective-permute-start | bytes 995336 | tf_op jit(solution)/shard_map/ppermute | solution.py:531
  146.5 14.5 %collective-permute-start.11 = (bf16[864,192]{0,1:T(8,128)(2,1)}, bf16[864,192]{0,1:T(8,128)(2,1)}, u32[]{:S(2)}, u32[]{:S(2)}) collective-permute-start(bf16[864,192]{0,1:T(8,128)(2,1)} %bitcast.268), channel_id=1, source_target_pairs={{0,12},{4,8},{8,4},{12,0},{16,28},{20,24},{24,20},{28,16},{1,13},{... | collective-permute-start | bytes 995336 | tf_op jit(solution)/shard_map/ppermute | solution.py:531
  171.4 35.4 %collective-permute-start.7 = (bf16[2,256,768]{2,1,0:T(8,128)(2,1)}, bf16[2,256,768]{2,1,0:T(8,128)(2,1)S(1)}, u32[]{:S(2)}, u32[]{:S(2)}) collective-permute-start(bf16[2,256,768]{2,1,0:T(8,128)(2,1)} %slice_select_fusion.2), channel_id=1, source_target_pairs={{0,1},{1,2},{2,3},{4,5},{5,6},{6,7},{8,9},{9,10},{10,11},{12,13},{... | collective-permute-start | bytes 2359304 | tf_op jit(solution)/shard_map/ppermute | solution.py:630
  205.3 29.8 %collective-permute-start.12 = (bf16[384,768]{1,0:T(8,128)(2,1)}, bf16[384,768]{1,0:T(8,128)(2,1)}, u32[]{:S(2)}, u32[]{:S(2)}) collective-permute-start(bf16[384,768]{1,0:T(8,128)(2,1)} %all_gather.24), channel_id=1, source_target_pairs={{0,16},{4,20},{8,24},{12,28},{16,0},{20,4},{24,8},{28,12},{1,17},{... | collective-permute-start | bytes 1769480 | tf_op jit(solution)/shard_map/ppermute | solution.py:531
  232.3 3.9 collective-permute-start.8
  233.9 75.3 %all-gather.11.cloned.1.call-start = ((), (), s32[]{:S(2)}) async-start(), calls=%async_computation.7 | async-start | bytes 1966080 | tf_op jit(solution)/shard_map/all_gather | solution.py:553
  243.2 5.0 collective-permute-start.13
  244.8 102.3 %all-gather.13.cloned.1.call-start = ((), (), s32[]{:S(2)}) async-start(), calls=%async_computation.8 | async-start | bytes 1966080 | tf_op jit(solution)/shard_map/all_gather | solution.py:553
  246.4 28.9 %collective-permute-start.22 = (bf16[384,1536]{1,0:T(8,128)(2,1)S(1)}, bf16[384,1536]{1,0:T(8,128)(2,1)S(1)}, u32[]{:S(2)}, u32[]{:S(2)}) collective-permute-start(bf16[384,1536]{1,0:T(8,128)(2,1)S(1)} %maximum_select_fusion.2), channel_id=1, source_target_pairs={{0,8},{4,12},{8,0},{12,4},{16,24},{20,28},{24,16},{28,20},{1,9},{5... | collective-permute-start | bytes 3538952 | tf_op jit(solution)/shard_map/ppermute | solution.py:531
  254.7 45.1 %collective-permute-start.14 = (bf16[384,1536]{1,0:T(8,128)(2,1)}, bf16[384,1536]{1,0:T(8,128)(2,1)}, u32[]{:S(2)}, u32[]{:S(2)}) collective-permute-start(bf16[384,1536]{1,0:T(8,128)(2,1)} %fusion.18), channel_id=1, source_target_pairs={{0,8},{4,12},{8,0},{12,4},{16,24},{20,28},{24,16},{28,20},{1,9},{5... | collective-permute-start | bytes 3538952 | tf_op jit(solution)/shard_map/ppermute | solution.py:531
  256.2 423.9 %reduce-scatter.14.cloned.1.call-start = ((), (), s32[]{:S(2)}) async-start(), calls=%async_computation.13 | async-start | bytes 1966080 | tf_op jit(solution)/shard_map/reduce_scatter | solution.py:694
  277.1 76.0 %collective-permute-start.23 = (bf16[2,384,1536]{2,1,0:T(8,128)(2,1)}, bf16[2,384,1536]{2,1,0:T(8,128)(2,1)}, u32[]{:S(2)}, u32[]{:S(2)}) collective-permute-start(bf16[2,384,1536]{2,1,0:T(8,128)(2,1)} %pad_maximum_fusion.6), channel_id=1, source_target_pairs={{0,4},{4,0},{8,12},{12,8},{16,20},{20,16},{24,28},{28,24},{1,5},{5... | collective-permute-start | bytes 7077896 | tf_op jit(solution)/shard_map/ppermute | solution.py:531
  302.9 46.0 %collective-permute-start.15 = (bf16[384,1536]{1,0:T(8,128)(2,1)}, bf16[384,1536]{1,0:T(8,128)(2,1)S(1)}, u32[]{:S(2)}, u32[]{:S(2)}) collective-permute-start(bf16[384,1536]{1,0:T(8,128)(2,1)} %multiply_convert_fusion.3), channel_id=1, source_target_pairs={{0,8},{4,12},{8,0},{12,4},{16,24},{20,28},{24,16},{28,20},{1,9},{5... | collective-permute-start | bytes 3538952 | tf_op jit(solution)/shard_map/ppermute | solution.py:531
  304.4 52.0 %collective-permute-start.17 = (bf16[1024,768]{0,1:T(8,128)(2,1)}, bf16[1024,768]{0,1:T(8,128)(2,1)}, u32[]{:S(2)}, u32[]{:S(2)}) collective-permute-start(bf16[1024,768]{0,1:T(8,128)(2,1)} %all-gather.9.cloned.1.call-done), channel_id=1, source_target_pairs={{0,16},{4,20},{8,24},{12,28},{16,0},{20,4},{24,8},{28,12},{1,17},{... | collective-permute-start | bytes 4718600 | tf_op jit(solution)/shard_map/ppermute | solution.py:531
  309.2 66.5 %collective-permute-start.18 = (bf16[1024,768]{0,1:T(8,128)(2,1)}, bf16[1024,768]{0,1:T(8,128)(2,1)}, u32[]{:S(2)}, u32[]{:S(2)}) collective-permute-start(bf16[1024,768]{0,1:T(8,128)(2,1)} %all-gather.11.cloned.1.call-done), channel_id=1, source_target_pairs={{0,16},{4,20},{8,24},{12,28},{16,0},{20,4},{24,8},{28,12},{1,17},{... | collective-permute-start | bytes 4718600 | tf_op jit(solution)/shard_map/ppermute | solution.py:531
  347.2 60.1 %collective-permute-start.19 = (bf16[1024,768]{0,1:T(8,128)(2,1)}, bf16[1024,768]{0,1:T(8,128)(2,1)S(1)}, u32[]{:S(2)}, u32[]{:S(2)}) collective-permute-start(bf16[1024,768]{0,1:T(8,128)(2,1)} %all-gather.13.cloned.1.call-done), channel_id=1, source_target_pairs={{0,16},{4,20},{8,24},{12,28},{16,0},{20,4},{24,8},{28,12},{1,17},{... | collective-permute-start | bytes 4718600 | tf_op jit(solution)/shard_map/ppermute | solution.py:531
  350.0 64.4 %collective-permute-start.16 = (bf16[2,384,1536]{2,1,0:T(8,128)(2,1)S(1)}, bf16[2,384,1536]{2,1,0:T(8,128)(2,1)S(1)}, u32[]{:S(2)}, u32[]{:S(2)}) collective-permute-start(bf16[2,384,1536]{2,1,0:T(8,128)(2,1)S(1)} %pad_maximum_fusion.5), channel_id=1, source_target_pairs={{0,4},{4,0},{8,12},{12,8},{16,20},{20,16},{24,28},{28,24},{1,5},{5... | collective-permute-start | bytes 7077896 | tf_op jit(solution)/shard_map/ppermute | solution.py:531
  443.4 34.4 %collective-permute-start.49 = (bf16[1024,768]{1,0:T(8,128)(2,1)S(1)}, bf16[1024,768]{1,0:T(8,128)(2,1)S(1)}, u32[]{:S(2)}, u32[]{:S(2)}) collective-permute-start(bf16[1024,768]{1,0:T(8,128)(2,1)S(1)} %slice.358), channel_id=1, source_target_pairs={{0,16},{4,20},{8,24},{12,28},{16,0},{20,4},{24,8},{28,12},{1,17},{... | collective-permute-start | bytes 4718600 | tf_op jit(solution)/shard_map/ppermute | solution.py:531
  463.8 15.6 %collective-permute-start.24 = (bf16[2,384,1536]{2,1,0:T(8,128)(2,1)}, bf16[2,384,1536]{2,1,0:T(8,128)(2,1)}, u32[]{:S(2)}, u32[]{:S(2)}) collective-permute-start(bf16[2,384,1536]{2,1,0:T(8,128)(2,1)} %bitcast.43), channel_id=1, source_target_pairs={{0,4},{4,0},{8,12},{12,8},{16,20},{20,16},{24,28},{28,24},{1,5},{5... | collective-permute-start | bytes 7077896 | tf_op jit(solution)/shard_map/ppermute | solution.py:531
  473.6 9.7 %collective-permute-start.20 = (bf16[2,384,1536]{2,1,0:T(8,128)(2,1)}, bf16[2,384,1536]{2,1,0:T(8,128)(2,1)}, u32[]{:S(2)}, u32[]{:S(2)}) collective-permute-start(bf16[2,384,1536]{2,1,0:T(8,128)(2,1)} %bitcast.36), channel_id=1, source_target_pairs={{0,4},{4,0},{8,12},{12,8},{16,20},{20,16},{24,28},{28,24},{1,5},{5... | collective-permute-start | bytes 7077896 | tf_op jit(solution)/shard_map/ppermute | solution.py:531
  479.4 204.6 %reduce-scatter.12.cloned.1.call-start = ((), (), s32[]{:S(2)}) async-start(), calls=%async_computation.12 | async-start | bytes 1966080 | tf_op jit(solution)/shard_map/reduce_scatter | solution.py:694
  482.7 28.9 %collective-permute-start.25 = (bf16[384,1536]{1,0:T(8,128)(2,1)S(1)}, bf16[384,1536]{1,0:T(8,128)(2,1)S(1)}, u32[]{:S(2)}, u32[]{:S(2)}) collective-permute-start(bf16[384,1536]{1,0:T(8,128)(2,1)S(1)} %fusion.20), channel_id=1, source_target_pairs={{0,8},{4,12},{8,0},{12,4},{16,24},{20,28},{24,16},{28,20},{1,9},{5... | collective-permute-start | bytes 3538952 | tf_op jit(solution)/shard_map/ppermute | solution.py:531
  487.3 45.8 %collective-permute-start.21 = (bf16[384,1536]{1,0:T(8,128)(2,1)S(1)}, bf16[384,1536]{1,0:T(8,128)(2,1)S(1)}, u32[]{:S(2)}, u32[]{:S(2)}) collective-permute-start(bf16[384,1536]{1,0:T(8,128)(2,1)S(1)} %fusion.19), channel_id=1, source_target_pairs={{0,8},{4,12},{8,0},{12,4},{16,24},{20,28},{24,16},{28,20},{1,9},{5... | collective-permute-start | bytes 3538952 | tf_op jit(solution)/shard_map/ppermute | solution.py:531
  493.6 42.9 %collective-permute-start.45 = (bf16[1024,768]{1,0:T(8,128)(2,1)S(1)}, bf16[1024,768]{1,0:T(8,128)(2,1)S(1)}, u32[]{:S(2)}, u32[]{:S(2)}) collective-permute-start(bf16[1024,768]{1,0:T(8,128)(2,1)S(1)} %slice.356), channel_id=1, source_target_pairs={{0,16},{4,20},{8,24},{12,28},{16,0},{20,4},{24,8},{28,12},{1,17},{... | collective-permute-start | bytes 4718600 | tf_op jit(solution)/shard_map/ppermute | solution.py:531
  535.9 24.4 %collective-permute-start.26 = (bf16[384,1536]{1,0:T(8,128)(2,1)}, bf16[384,1536]{1,0:T(8,128)(2,1)S(1)}, u32[]{:S(2)}, u32[]{:S(2)}) collective-permute-start(bf16[384,1536]{1,0:T(8,128)(2,1)} %get-tuple-element.41), channel_id=1, source_target_pairs={{0,8},{4,12},{8,0},{12,4},{16,24},{20,28},{24,16},{28,20},{1,9},{5... | collective-permute-start | bytes 3538952 | tf_op jit(solution)/shard_map/ppermute | solution.py:531
  538.1 148.4 %reduce-scatter.10.cloned.1.call-start = ((), (), s32[]{:S(2)}) async-start(), calls=%async_computation.11 | async-start | bytes 1966080 | tf_op jit(solution)/shard_map/reduce_scatter | solution.py:694
  562.0 46.6 %collective-permute-start.27 = (bf16[2,384,1536]{2,1,0:T(8,128)(2,1)S(1)}, bf16[2,384,1536]{2,1,0:T(8,128)(2,1)}, u32[]{:S(2)}, u32[]{:S(2)}) collective-permute-start(bf16[2,384,1536]{2,1,0:T(8,128)(2,1)S(1)} %pad_maximum_fusion.7), channel_id=1, source_target_pairs={{0,4},{4,0},{8,12},{12,8},{16,20},{20,16},{24,28},{28,24},{1,5},{5... | collective-permute-start | bytes 7077896 | tf_op jit(solution)/shard_map/ppermute | solution.py:531
  570.5 36.3 %collective-permute-start.41 = (bf16[1024,768]{1,0:T(8,128)(2,1)S(1)}, bf16[1024,768]{1,0:T(8,128)(2,1)S(1)}, u32[]{:S(2)}, u32[]{:S(2)}) collective-permute-start(bf16[1024,768]{1,0:T(8,128)(2,1)S(1)} %slice.354), channel_id=1, source_target_pairs={{0,16},{4,20},{8,24},{12,28},{16,0},{20,4},{24,8},{28,12},{1,17},{... | collective-permute-start | bytes 4718600 | tf_op jit(solution)/shard_map/ppermute | solution.py:531
  608.5 131.0 %reduce-scatter.8.cloned.1.call-start = ((), (), s32[]{:S(2)}) async-start(), calls=%async_computation.10 | async-start | bytes 737280 | tf_op jit(solution)/shard_map/reduce_scatter | solution.py:694
  614.8 5.0 collective-permute-start.28
  648.9 21.1 %collective-permute-start.29 = (bf16[2,256,768]{2,1,0:T(8,128)(2,1)}, bf16[2,256,768]{2,1,0:T(8,128)(2,1)S(1)}, u32[]{:S(2)}, u32[]{:S(2)}) collective-permute-start(bf16[2,256,768]{2,1,0:T(8,128)(2,1)} %get-tuple-element.18), channel_id=1, source_target_pairs={{1,0},{2,1},{3,2},{5,4},{6,5},{7,6},{9,8},{10,9},{11,10},{13,12},{... | collective-permute-start | bytes 2359304 | tf_op jit(solution)/shard_map/ppermute | solution.py:676
  678.7 9.8 %collective-permute-start.30 = (bf16[2,384,768]{2,1,0:T(8,128)(2,1)}, bf16[2,384,768]{2,1,0:T(8,128)(2,1)}, u32[]{:S(2)}, u32[]{:S(2)}) collective-permute-start(bf16[2,384,768]{2,1,0:T(8,128)(2,1)} %get-tuple-element.59), channel_id=1, source_target_pairs={{0,4},{4,0},{8,12},{12,8},{16,20},{20,16},{24,28},{28,24},{1,5},{5... | collective-permute-start | bytes 3538952 | tf_op jit(solution)/shard_map/ppermute | solution.py:531
  682.1 20.0 %collective-permute-start.50 = (bf16[256,192]{0,1:T(8,128)(2,1)}, bf16[256,192]{0,1:T(8,128)(2,1)}, u32[]{:S(2)}, u32[]{:S(2)}) collective-permute-start(bf16[256,192]{0,1:T(8,128)(2,1)} %get-tuple-element.99), channel_id=1, source_target_pairs={{0,4},{4,0},{8,12},{12,8},{16,20},{20,16},{24,28},{28,24},{1,5},{5... | collective-permute-start | bytes 294920 | tf_op jit(solution)/shard_map/ppermute | solution.py:531
  682.6 20.7 %collective-permute-start.51 = (bf16[256,192]{0,1:T(8,128)(2,1)}, bf16[256,192]{0,1:T(8,128)(2,1)}, u32[]{:S(2)}, u32[]{:S(2)}) collective-permute-start(bf16[256,192]{0,1:T(8,128)(2,1)} %get-tuple-element.98), channel_id=1, source_target_pairs={{0,8},{4,12},{8,0},{12,4},{16,24},{20,28},{24,16},{28,20},{1,9},{5... | collective-permute-start | bytes 294920 | tf_op jit(solution)/shard_map/ppermute | solution.py:531
  683.1 20.6 %collective-permute-start.52 = (bf16[256,192]{0,1:T(8,128)(2,1)}, bf16[256,192]{0,1:T(8,128)(2,1)}, u32[]{:S(2)}, u32[]{:S(2)}) collective-permute-start(bf16[256,192]{0,1:T(8,128)(2,1)} %get-tuple-element.97), channel_id=1, source_target_pairs={{0,12},{4,8},{8,4},{12,0},{16,28},{20,24},{24,20},{28,16},{1,13},{... | collective-permute-start | bytes 294920 | tf_op jit(solution)/shard_map/ppermute | solution.py:531
  685.9 19.5 %collective-permute-start.47 = (bf16[256,192]{0,1:T(8,128)(2,1)}, bf16[256,192]{0,1:T(8,128)(2,1)}, u32[]{:S(2)}, u32[]{:S(2)}) collective-permute-start(bf16[256,192]{0,1:T(8,128)(2,1)} %get-tuple-element.106), channel_id=1, source_target_pairs={{0,8},{4,12},{8,0},{12,4},{16,24},{20,28},{24,16},{28,20},{1,9},{5... | collective-permute-start | bytes 294920 | tf_op jit(solution)/shard_map/ppermute | solution.py:531
  697.4 31.3 %collective-permute-start.31 = (bf16[2,384,1536]{2,1,0:T(8,128)(2,1)}, bf16[2,384,1536]{2,1,0:T(8,128)(2,1)}, u32[]{:S(2)}, u32[]{:S(2)}) collective-permute-start(bf16[2,384,1536]{2,1,0:T(8,128)(2,1)} %bitcast.53), channel_id=1, source_target_pairs={{0,4},{4,0},{8,12},{12,8},{16,20},{20,16},{24,28},{28,24},{1,5},{5... | collective-permute-start | bytes 7077896 | tf_op jit(solution)/shard_map/ppermute | solution.py:531
  702.0 4.8 collective-permute-start.48
  703.3 5.2 collective-permute-start.46
  703.7 15.3 %collective-permute-start.37 = (bf16[384,768]{1,0:T(8,128)(2,1)S(1)}, bf16[384,768]{1,0:T(8,128)(2,1)S(1)}, u32[]{:S(2)}, u32[]{:S(2)}) collective-permute-start(bf16[384,768]{1,0:T(8,128)(2,1)S(1)} %slice.352), channel_id=1, source_target_pairs={{0,16},{4,20},{8,24},{12,28},{16,0},{20,4},{24,8},{28,12},{1,17},{... | collective-permute-start | bytes 1769480 | tf_op jit(solution)/shard_map/ppermute | solution.py:531
  705.4 29.6 %collective-permute-start.42 = (bf16[256,192]{0,1:T(8,128)(2,1)}, bf16[256,192]{0,1:T(8,128)(2,1)}, u32[]{:S(2)}, u32[]{:S(2)}) collective-permute-start(bf16[256,192]{0,1:T(8,128)(2,1)} %get-tuple-element.115), channel_id=1, source_target_pairs={{0,4},{4,0},{8,12},{12,8},{16,20},{20,16},{24,28},{28,24},{1,5},{5... | collective-permute-start | bytes 294920 | tf_op jit(solution)/shard_map/ppermute | solution.py:531
  706.9 28.1 %collective-permute-start.43 = (bf16[256,192]{0,1:T(8,128)(2,1)}, bf16[256,192]{0,1:T(8,128)(2,1)}, u32[]{:S(2)}, u32[]{:S(2)}) collective-permute-start(bf16[256,192]{0,1:T(8,128)(2,1)} %get-tuple-element.114), channel_id=1, source_target_pairs={{0,8},{4,12},{8,0},{12,4},{16,24},{20,28},{24,16},{28,20},{1,9},{5... | collective-permute-start | bytes 294920 | tf_op jit(solution)/shard_map/ppermute | solution.py:531
  708.5 26.5 %collective-permute-start.44 = (bf16[256,192]{0,1:T(8,128)(2,1)}, bf16[256,192]{0,1:T(8,128)(2,1)}, u32[]{:S(2)}, u32[]{:S(2)}) collective-permute-start(bf16[256,192]{0,1:T(8,128)(2,1)} %get-tuple-element.113), channel_id=1, source_target_pairs={{0,12},{4,8},{8,4},{12,0},{16,28},{20,24},{24,20},{28,16},{1,13},{... | collective-permute-start | bytes 294920 | tf_op jit(solution)/shard_map/ppermute | solution.py:531
  720.0 95.9 %reduce-scatter.6.cloned.1.call-start = ((), (), s32[]{:S(2)}) async-start(), calls=%async_computation.9 | async-start | bytes 1474560 | tf_op jit(solution)/shard_map/reduce_scatter | solution.py:694
  728.1 35.8 %collective-permute-start.33 = (bf16[768,768]{1,0:T(8,128)(2,1)}, bf16[768,768]{1,0:T(8,128)(2,1)}, u32[]{:S(2)}, u32[]{:S(2)}) collective-permute-start(bf16[768,768]{1,0:T(8,128)(2,1)} %slice.350), channel_id=1, source_target_pairs={{0,16},{4,20},{8,24},{12,28},{16,0},{20,4},{24,8},{28,12},{1,17},{... | collective-permute-start | bytes 3538952 | tf_op jit(solution)/shard_map/ppermute | solution.py:531
  734.4 32.3 %collective-permute-start.32 = (bf16[384,1536]{1,0:T(8,128)(2,1)}, bf16[384,1536]{1,0:T(8,128)(2,1)}, u32[]{:S(2)}, u32[]{:S(2)}) collective-permute-start(bf16[384,1536]{1,0:T(8,128)(2,1)} %fusion.21), channel_id=1, source_target_pairs={{0,8},{4,12},{8,0},{12,4},{16,24},{20,28},{24,16},{28,20},{1,9},{5... | collective-permute-start | bytes 3538952 | tf_op jit(solution)/shard_map/ppermute | solution.py:531
  741.1 3.1 collective-permute-start.38
  741.2 21.8 %collective-permute-start.39 = (bf16[96,192]{1,0:T(8,128)(2,1)S(1)}, bf16[96,192]{1,0:T(8,128)(2,1)S(1)}, u32[]{:S(2)}, u32[]{:S(2)}) collective-permute-start(bf16[96,192]{1,0:T(8,128)(2,1)S(1)} %bitcast.340), channel_id=1, source_target_pairs={{0,8},{4,12},{8,0},{12,4},{16,24},{20,28},{24,16},{28,20},{1,9},{5... | collective-permute-start | bytes 110600 | tf_op jit(solution)/shard_map/ppermute | solution.py:531
  742.7 20.3 %collective-permute-start.40 = (bf16[96,192]{1,0:T(8,128)(2,1)S(1)}, bf16[96,192]{1,0:T(8,128)(2,1)S(1)}, u32[]{:S(2)}, u32[]{:S(2)}) collective-permute-start(bf16[96,192]{1,0:T(8,128)(2,1)S(1)} %bitcast.341), channel_id=1, source_target_pairs={{0,12},{4,8},{8,4},{12,0},{16,28},{20,24},{24,20},{28,16},{1,13},{... | collective-permute-start | bytes 110600 | tf_op jit(solution)/shard_map/ppermute | solution.py:531
  818.1 4.1 collective-permute-start.34
  818.2 6.0 collective-permute-start.35
  820.6 5.3 collective-permute-start.36
  (76 other events, 669.4 us)
Sparse Core Ops, SparseCore 0:
  60.4 30.6 all-gather.6
  234.1 37.5 all-gather.8
  273.3 35.9 all-gather.10
  311.2 35.9 all-gather.12
  479.5 34.2 reduce-scatter.13
  538.2 35.2 reduce-scatter.11
  608.7 34.3 reduce-scatter.9
  720.1 19.3 reduce-scatter.7
  766.8 27.8 reduce-scatter.5
